TPU v7x, 32 devices: a whole 2x2x4 slice. The times are simulated.
32 devices in a mesh: pair: 4 (over y, x), side: 2 (over core), blk: 4 (over z).
Axes of the slice: x: 2, y: 2, z: 4, core: 2. Of those that a mesh axis runs over, the one named last changes fastest.
Arguments:
- intersect: float32 [4096, 768], P(('pair', 'side', 'blk')), parts along dimension 0, may hold values from -0.1 to 1.7, as said below
- half_factors: float32 [4096, 384], P(('pair', 'side', 'blk')), parts along dimension 0, may hold values from -0.03 to 1.35, as said below
- z_pattern: int32 [32, 6], P(('pair', 'side', 'blk')), parts along dimension 0, may hold values 0 or 1
Outputs:
- refined_factor: float32 [4096, 768], P(('pair', 'side', 'blk')), parts along dimension 0
There are 4 independent parts, one for each index of `pair`. A program takes and returns all parts, laid end to end along the dimension named above; each array names one. Nothing has to cross between parts.
Inputs may be any that keep to these rules, and one draw needn't show every extreme that they name: As a whole windowed matrix, intersect is symmetric: S[a, b] = S[b, a]. `half_factors`: entries of the other half and outside the grid of blocks are absent or zero. `z_pattern`: 1 keeps a tile of the factor, 0 drops it; diagonal tiles are kept whatever it says.
All inputs are finite; a program needn't handle non-finite values. No bound on the sum of `z_pattern` on one device may be relied on, other than what follows from the above.
Results may differ from a plain program's by a relative error of at most 0.0001.
Values sent between devices are 32-bit elements; how exact they have to be, the bound alone decides.
No kernel may reach another device: no remote copies, remote signals or barrier semaphores. Data moves between devices by JAX's collectives and lax.ppermute only.
A program may use at most 64 MiB of HBM per device.

v0:
```python
import jax
import jax.numpy as jnp
from jax import lax
from jax.sharding import PartitionSpec as P

ITERS = 2


def padded(cells, sides, width):
    for axis, dim in sides:
        count = lax.axis_size(axis)
        ends = count - 1
        head = lax.slice_in_dim(cells, 0, width, axis=dim)
        tail = lax.slice_in_dim(cells, cells.shape[dim] - width, cells.shape[dim], axis=dim)
        cells = jnp.concatenate(
            [
                lax.ppermute(tail, axis, [(i, (i + 1) % count) for i in range(ends)]),
                cells,
                lax.ppermute(head, axis, [((i + 1) % count, i) for i in range(ends)]),
            ],
            axis=dim,
        )
    return cells


def swapped(block, axis, stride):
    count = lax.axis_size(axis)
    route = []
    for low in range(count):
        high = low | 1 << stride
        if high != low and high < count:
            route += [(low, high), (high, low)]
    return lax.ppermute(block, axis, route)


def near_blocks(panel):
    return padded(panel[None], (("blk", 0),), 1)


def neighbours(panel):
    side = lax.axis_index("side")
    local = near_blocks(panel)
    other = swapped(local, "side", 0)
    return jnp.stack((jnp.where(side == 0, local, other), jnp.where(side == 0, other, local)))


def window_product(left, nearby):
    outputs = []
    for target in range(3):
        total = None
        for slot in range(3):
            source = target + 1 - slot
            if 0 <= source <= 2:
                term = lax.dot_general(
                    left[:, slot],
                    nearby[:, slot, :, source],
                    (((1, 2), (0, 1)), ((), ())),
                    precision=lax.Precision.HIGHEST,
                    preferred_element_type=jnp.float32,
                )
                total = term if total is None else total + term
        outputs.append(total)
    return jnp.stack(outputs, axis=1)


def window_cross(near_factor, near_image, side):
    mines = []
    for slot in range(3):
        column = near_factor[:, slot, :, 2 - slot]
        mines.append(lax.dynamic_index_in_dim(column, side, axis=2, keepdims=False))
    outputs = []
    for target in range(3):
        total = None
        for slot in range(3):
            source = target + 1 - slot
            if 0 <= source <= 2:
                term = lax.dot_general(
                    mines[slot],
                    near_image[:, slot, :, source],
                    (((0, 1), (0, 1)), ((), ())),
                    precision=lax.Precision.HIGHEST,
                    preferred_element_type=jnp.float32,
                )
                total = term if total is None else total + term
        outputs.append(total)
    return jnp.stack(outputs, axis=1)


def window_keep(pattern, tile, side):
    count = pattern.shape[0]
    grid = pattern.reshape(count, 3, 2, count)
    slots = jnp.arange(3)[None, :, None, None]
    halves = jnp.arange(2)[None, None, :, None]
    row_tiles = jnp.arange(count)[:, None, None, None]
    col_tiles = jnp.arange(count)[None, None, None, :]
    diagonal = ((slots == 1) & (halves == side) & (row_tiles == col_tiles)).astype(jnp.int32)
    kept = jnp.maximum(grid, diagonal).astype(jnp.float32)
    wide = jnp.broadcast_to(kept[:, None, :, :, :, None], (count, tile, 3, 2, count, tile))
    return wide.reshape(count * tile, 3, 2, count * tile)


def per_device(intersect, half_factors, z_pattern):
    rows = intersect.shape[0]
    tile = rows // z_pattern.shape[0]
    side = lax.axis_index("side")
    eye_side = jnp.eye(2, dtype=jnp.float32)
    own_side = (jnp.arange(2) == side).astype(jnp.float32)
    intersect_win = intersect.reshape(rows, 3, 2, rows)
    keep = window_keep(z_pattern, tile, side)
    slots = jnp.arange(3)[None, :, None, None]
    halves = jnp.arange(2)[None, None, :, None]
    row_ids = jnp.arange(rows)[:, None, None, None]
    col_ids = jnp.arange(rows)[None, None, None, :]
    identity = ((slots == 1) & (halves == side) & (row_ids == col_ids)).astype(jnp.float32)
    half_win = half_factors.reshape(rows, 3, rows)
    factor = half_win[:, :, None, :] * own_side[None, None, :, None]
    near_half = neighbours(half_factors).reshape(2, 3, rows, 3, rows)
    near_factor = near_half[:, :, :, :, None, :] * eye_side[:, None, None, None, :, None]
    for step in range(ITERS):
        if step > 0:
            near_factor = neighbours(factor.reshape(rows, 6 * rows)).reshape(2, 3, rows, 3, 2, rows)
        image = window_product(intersect_win, near_factor)
        near_image = neighbours(image.reshape(rows, 6 * rows)).reshape(2, 3, rows, 3, 2, rows)
        delta = identity - window_cross(near_factor, near_image, side)
        near_delta = neighbours(delta.reshape(rows, 6 * rows)).reshape(2, 3, rows, 3, 2, rows)
        first = window_product(factor, near_delta)
        second = window_product(first, near_delta)
        factor = keep * (factor + 0.5 * first + 0.375 * second)
    return factor.reshape(rows, 6 * rows)


def solution(mesh):
    return jax.shard_map(
        per_device,
        mesh=mesh,
        in_specs=(
            P(("pair", "side", "blk"), None),
            P(("pair", "side", "blk"), None),
            P(("pair", "side", "blk"), None),
        ),
        out_specs=P(("pair", "side", "blk"), None),
        check_vma=False,
    )
```

profile of v0, /device:TPU:29, one launch (start us, length us, event | category | flops | bytes accessed | tf_op | source)
XLA Modules:
  0.0 135.1 jit_solution(8371497596822709502)
XLA Ops:
  1.1 2.1 %collective-permute-start.1 = (f32[1,128,384]{1,2,0:T(8,128)S(1)}, f32[1,128,384]{1,2,0:T(8,128)S(1)}, u32[]{:S(2)}, u32[]{:S(2)}) collective-permute-start(f32[1,128,384]{1,2,0:T(8,128)S(1)} %bitcast.698), channel_id=1, source_target_pairs={{1,0},{2,1},{3,2},{5,4},{6,5},{7,6},{9,8},{10,9},{11,10},{13,12},{... | collective-permute-start | bytes 589832 | tf_op jit(solution)/shard_map/ppermute | solution.py:19
  4.5 2.3 %collective-permute-done.1 = f32[1,128,384]{1,2,0:T(8,128)S(1)} collective-permute-done((f32[1,128,384]{1,2,0:T(8,128)S(1)}, f32[1,128,384]{1,2,0:T(8,128)S(1)}, u32[]{:S(2)}, u32[]{:S(2)}) %collective-permute-start.1) | collective-permute-done | bytes 196640 | tf_op jit(solution)/shard_map/ppermute | solution.py:19
  6.8 3.8 %collective-permute-done = f32[1,128,384]{1,2,0:T(8,128)S(1)} collective-permute-done((f32[1,128,384]{1,2,0:T(8,128)S(1)}, f32[1,128,384]{1,2,0:T(8,128)S(1)}, u32[]{:S(2)}, u32[]{:S(2)}) %collective-permute-start) | collective-permute-done | bytes 196640 | tf_op jit(solution)/shard_map/ppermute | solution.py:17
  10.6 1.9 %collective-permute-start.2 = (f32[3,128,384]{1,2,0:T(8,128)S(1)}, f32[3,128,384]{1,2,0:T(8,128)S(1)}, u32[]{:S(2)}, u32[]{:S(2)}) collective-permute-start(f32[3,128,384]{1,2,0:T(8,128)S(1)} %pad_maximum_fusion.5), channel_id=1, source_target_pairs={{0,4},{4,0},{1,5},{5,1},{2,6},{6,2},{3,7},{7,3},{8,12},{12,8},{9,1... | collective-permute-start | bytes 1769480 | tf_op jit(solution)/shard_map/ppermute | solution.py:33
  17.3 2.1 %collective-permute-start.4 = (f32[1,128,768]{1,2,0:T(8,128)S(1)}, f32[1,128,768]{1,2,0:T(8,128)S(1)}, u32[]{:S(2)}, u32[]{:S(2)}) collective-permute-start(f32[1,128,768]{1,2,0:T(8,128)S(1)} %bitcast.709), channel_id=1, source_target_pairs={{1,0},{2,1},{3,2},{5,4},{6,5},{7,6},{9,8},{10,9},{11,10},{13,12},{... | collective-permute-start | bytes 1179656 | tf_op jit(solution)/shard_map/ppermute | solution.py:19
  20.7 6.8 %collective-permute-done.4 = f32[1,128,768]{1,2,0:T(8,128)S(1)} collective-permute-done((f32[1,128,768]{1,2,0:T(8,128)S(1)}, f32[1,128,768]{1,2,0:T(8,128)S(1)}, u32[]{:S(2)}, u32[]{:S(2)}) %collective-permute-start.4) | collective-permute-done | bytes 393248 | tf_op jit(solution)/shard_map/ppermute | solution.py:19
  27.5 3.9 %collective-permute-done.3 = f32[1,128,768]{1,2,0:T(8,128)S(1)} collective-permute-done((f32[1,128,768]{1,2,0:T(8,128)S(1)}, f32[1,128,768]{1,2,0:T(8,128)S(1)}, u32[]{:S(2)}, u32[]{:S(2)}) %collective-permute-start.3) | collective-permute-done | bytes 393248 | tf_op jit(solution)/shard_map/ppermute | solution.py:17
  41.3 2.1 %collective-permute-start.7 = (f32[1,128,768]{1,2,0:T(8,128)S(1)}, f32[1,128,768]{1,2,0:T(8,128)S(1)}, u32[]{:S(2)}, u32[]{:S(2)}) collective-permute-start(f32[1,128,768]{1,2,0:T(8,128)S(1)} %convert_subtract_fusion.1), channel_id=1, source_target_pairs={{1,0},{2,1},{3,2},{5,4},{6,5},{7,6},{9,8},{10,9},{11,10},{13,12},{... | collective-permute-start | bytes 1179656 | tf_op jit(solution)/shard_map/ppermute | solution.py:19
  44.9 6.6 %collective-permute-done.7 = f32[1,128,768]{1,2,0:T(8,128)S(1)} collective-permute-done((f32[1,128,768]{1,2,0:T(8,128)S(1)}, f32[1,128,768]{1,2,0:T(8,128)S(1)}, u32[]{:S(2)}, u32[]{:S(2)}) %collective-permute-start.7) | collective-permute-done | bytes 393248 | tf_op jit(solution)/shard_map/ppermute | solution.py:19
  51.4 3.9 %collective-permute-done.6 = f32[1,128,768]{1,2,0:T(8,128)S(1)} collective-permute-done((f32[1,128,768]{1,2,0:T(8,128)S(1)}, f32[1,128,768]{1,2,0:T(8,128)S(1)}, u32[]{:S(2)}, u32[]{:S(2)}) %collective-permute-start.6) | collective-permute-done | bytes 393248 | tf_op jit(solution)/shard_map/ppermute | solution.py:17
  58.3 2.3 %collective-permute-done.8 = f32[3,128,768]{1,2,0:T(8,128)S(1)} collective-permute-done((f32[3,128,768]{1,2,0:T(8,128)}, f32[3,128,768]{1,2,0:T(8,128)S(1)}, u32[]{:S(2)}, u32[]{:S(2)}) %collective-permute-start.8) | collective-permute-done | bytes 1179680 | tf_op jit(solution)/shard_map/ppermute | solution.py:33
  67.4 1.9 %collective-permute-start.10 = (f32[1,128,768]{1,2,0:T(8,128)S(1)}, f32[1,128,768]{1,2,0:T(8,128)S(1)}, u32[]{:S(2)}, u32[]{:S(2)}) collective-permute-start(f32[1,128,768]{1,2,0:T(8,128)S(1)} %add_multiply_fusion), channel_id=1, source_target_pairs={{1,0},{2,1},{3,2},{5,4},{6,5},{7,6},{9,8},{10,9},{11,10},{13,12},{... | collective-permute-start | bytes 1179656 | tf_op jit(solution)/shard_map/ppermute | solution.py:19
  70.6 6.8 %collective-permute-done.10 = f32[1,128,768]{1,2,0:T(8,128)S(1)} collective-permute-done((f32[1,128,768]{1,2,0:T(8,128)S(1)}, f32[1,128,768]{1,2,0:T(8,128)S(1)}, u32[]{:S(2)}, u32[]{:S(2)}) %collective-permute-start.10) | collective-permute-done | bytes 393248 | tf_op jit(solution)/shard_map/ppermute | solution.py:19
  77.4 3.9 %collective-permute-done.9 = f32[1,128,768]{1,2,0:T(8,128)S(1)} collective-permute-done((f32[1,128,768]{1,2,0:T(8,128)S(1)}, f32[1,128,768]{1,2,0:T(8,128)S(1)}, u32[]{:S(2)}, u32[]{:S(2)}) %collective-permute-start.9) | collective-permute-done | bytes 393248 | tf_op jit(solution)/shard_map/ppermute | solution.py:17
  81.3 1.6 %collective-permute-start.11 = (f32[3,128,768]{1,2,0:T(8,128)S(1)}, f32[3,128,768]{1,2,0:T(8,128)S(1)}, u32[]{:S(2)}, u32[]{:S(2)}) collective-permute-start(f32[3,128,768]{1,2,0:T(8,128)S(1)} %pad_maximum_fusion.2), channel_id=1, source_target_pairs={{0,4},{4,0},{1,5},{5,1},{2,6},{6,2},{3,7},{7,3},{8,12},{12,8},{9,1... | collective-permute-start | bytes 3538952 | tf_op jit(solution)/shard_map/ppermute | solution.py:33
  82.9 2.5 %collective-permute-done.11 = f32[3,128,768]{1,2,0:T(8,128)S(1)} collective-permute-done((f32[3,128,768]{1,2,0:T(8,128)S(1)}, f32[3,128,768]{1,2,0:T(8,128)S(1)}, u32[]{:S(2)}, u32[]{:S(2)}) %collective-permute-start.11) | collective-permute-done | bytes 1179680 | tf_op jit(solution)/shard_map/ppermute | solution.py:33
  88.4 1.9 %collective-permute-start.13 = (f32[1,128,768]{1,2,0:T(8,128)S(1)}, f32[1,128,768]{1,2,0:T(8,128)S(1)}, u32[]{:S(2)}, u32[]{:S(2)}) collective-permute-start(f32[1,128,768]{1,2,0:T(8,128)S(1)} %bitcast.713), channel_id=1, source_target_pairs={{1,0},{2,1},{3,2},{5,4},{6,5},{7,6},{9,8},{10,9},{11,10},{13,12},{... | collective-permute-start | bytes 1179656 | tf_op jit(solution)/shard_map/ppermute | solution.py:19
  91.6 6.8 %collective-permute-done.13 = f32[1,128,768]{1,2,0:T(8,128)S(1)} collective-permute-done((f32[1,128,768]{1,2,0:T(8,128)S(1)}, f32[1,128,768]{1,2,0:T(8,128)S(1)}, u32[]{:S(2)}, u32[]{:S(2)}) %collective-permute-start.13) | collective-permute-done | bytes 393248 | tf_op jit(solution)/shard_map/ppermute | solution.py:19
  98.4 3.9 %collective-permute-done.12 = f32[1,128,768]{1,2,0:T(8,128)S(1)} collective-permute-done((f32[1,128,768]{1,2,0:T(8,128)S(1)}, f32[1,128,768]{1,2,0:T(8,128)S(1)}, u32[]{:S(2)}, u32[]{:S(2)}) %collective-permute-start.12) | collective-permute-done | bytes 393248 | tf_op jit(solution)/shard_map/ppermute | solution.py:17
  103.9 2.5 %collective-permute-done.14 = f32[3,128,768]{1,2,0:T(8,128)S(1)} collective-permute-done((f32[3,128,768]{1,2,0:T(8,128)S(1)}, f32[3,128,768]{1,2,0:T(8,128)S(1)}, u32[]{:S(2)}, u32[]{:S(2)}) %collective-permute-start.14) | collective-permute-done | bytes 1179680 | tf_op jit(solution)/shard_map/ppermute | solution.py:33
  109.5 1.9 %collective-permute-start.16 = (f32[1,128,768]{1,2,0:T(8,128)S(1)}, f32[1,128,768]{1,2,0:T(8,128)S(1)}, u32[]{:S(2)}, u32[]{:S(2)}) collective-permute-start(f32[1,128,768]{1,2,0:T(8,128)S(1)} %convert_subtract_fusion), channel_id=1, source_target_pairs={{1,0},{2,1},{3,2},{5,4},{6,5},{7,6},{9,8},{10,9},{11,10},{13,12},{... | collective-permute-start | bytes 1179656 | tf_op jit(solution)/shard_map/ppermute | solution.py:19
  112.9 6.5 %collective-permute-done.16 = f32[1,128,768]{1,2,0:T(8,128)S(1)} collective-permute-done((f32[1,128,768]{1,2,0:T(8,128)S(1)}, f32[1,128,768]{1,2,0:T(8,128)S(1)}, u32[]{:S(2)}, u32[]{:S(2)}) %collective-permute-start.16) | collective-permute-done | bytes 393248 | tf_op jit(solution)/shard_map/ppermute | solution.py:19
  119.5 3.9 %collective-permute-done.15 = f32[1,128,768]{1,2,0:T(8,128)S(1)} collective-permute-done((f32[1,128,768]{1,2,0:T(8,128)S(1)}, f32[1,128,768]{1,2,0:T(8,128)S(1)}, u32[]{:S(2)}, u32[]{:S(2)}) %collective-permute-start.15) | collective-permute-done | bytes 393248 | tf_op jit(solution)/shard_map/ppermute | solution.py:17
  125.0 2.5 %collective-permute-done.17 = f32[3,128,768]{1,2,0:T(8,128)S(1)} collective-permute-done((f32[3,128,768]{1,2,0:T(8,128)S(1)}, f32[3,128,768]{1,2,0:T(8,128)S(1)}, u32[]{:S(2)}, u32[]{:S(2)}) %collective-permute-start.17) | collective-permute-done | bytes 1179680 | tf_op jit(solution)/shard_map/ppermute | solution.py:33
  (135 shorter events, 50.4 us)
Async XLA Ops:
  0.0 12.5 %copy-start.4 = (f32[128,768]{1,0:T(8,128)S(1)}, f32[128,768]{1,0:T(8,128)}, u32[]{:S(2)}) copy-start(f32[128,768]{1,0:T(8,128)} %param.3) | copy-start | bytes 1179652
  1.1 5.6 %collective-permute-start.1 = (f32[1,128,384]{1,2,0:T(8,128)S(1)}, f32[1,128,384]{1,2,0:T(8,128)S(1)}, u32[]{:S(2)}, u32[]{:S(2)}) collective-permute-start(f32[1,128,384]{1,2,0:T(8,128)S(1)} %bitcast.698), channel_id=1, source_target_pairs={{1,0},{2,1},{3,2},{5,4},{6,5},{7,6},{9,8},{10,9},{11,10},{13,12},{... | collective-permute-start | bytes 589832 | tf_op jit(solution)/shard_map/ppermute | solution.py:19
  3.2 7.4 %collective-permute-start = (f32[1,128,384]{1,2,0:T(8,128)S(1)}, f32[1,128,384]{1,2,0:T(8,128)S(1)}, u32[]{:S(2)}, u32[]{:S(2)}) collective-permute-start(f32[1,128,384]{1,2,0:T(8,128)S(1)} %bitcast.699), channel_id=1, source_target_pairs={{0,1},{1,2},{2,3},{4,5},{5,6},{6,7},{8,9},{9,10},{10,11},{12,13},{... | collective-permute-start | bytes 589832 | tf_op jit(solution)/shard_map/ppermute | solution.py:17
  10.6 3.5 %collective-permute-start.2 = (f32[3,128,384]{1,2,0:T(8,128)S(1)}, f32[3,128,384]{1,2,0:T(8,128)S(1)}, u32[]{:S(2)}, u32[]{:S(2)}) collective-permute-start(f32[3,128,384]{1,2,0:T(8,128)S(1)} %pad_maximum_fusion.5), channel_id=1, source_target_pairs={{0,4},{4,0},{1,5},{5,1},{2,6},{6,2},{3,7},{7,3},{8,12},{12,8},{9,1... | collective-permute-start | bytes 1769480 | tf_op jit(solution)/shard_map/ppermute | solution.py:33
  17.3 17.3 %copy-start.5 = (s32[1,6]{1,0:T(1,128)S(1)}, s32[1,6]{1,0:T(1,128)}, u32[]{:S(2)}) copy-start(s32[1,6]{1,0:T(1,128)} %param.5) | copy-start | bytes 76
  17.3 10.2 %collective-permute-start.4 = (f32[1,128,768]{1,2,0:T(8,128)S(1)}, f32[1,128,768]{1,2,0:T(8,128)S(1)}, u32[]{:S(2)}, u32[]{:S(2)}) collective-permute-start(f32[1,128,768]{1,2,0:T(8,128)S(1)} %bitcast.709), channel_id=1, source_target_pairs={{1,0},{2,1},{3,2},{5,4},{6,5},{7,6},{9,8},{10,9},{11,10},{13,12},{... | collective-permute-start | bytes 1179656 | tf_op jit(solution)/shard_map/ppermute | solution.py:19
  19.4 11.9 %collective-permute-start.3 = (f32[1,128,768]{1,2,0:T(8,128)S(1)}, f32[1,128,768]{1,2,0:T(8,128)S(1)}, u32[]{:S(2)}, u32[]{:S(2)}) collective-permute-start(f32[1,128,768]{1,2,0:T(8,128)S(1)} %bitcast.710), channel_id=1, source_target_pairs={{0,1},{1,2},{2,3},{4,5},{5,6},{6,7},{8,9},{9,10},{10,11},{12,13},{... | collective-permute-start | bytes 1179656 | tf_op jit(solution)/shard_map/ppermute | solution.py:17
  27.5 5.0 %copy-start = (f32[1,128,768]{1,2,0:T(8,128)}, f32[1,128,768]{1,2,0:T(8,128)S(1)}, u32[]{:S(2)}) copy-start(f32[1,128,768]{1,2,0:T(8,128)S(1)} %collective-permute-done.4) | copy-start | bytes 1179652
  31.3 1.2 copy-start.2
  32.5 4.3 %collective-permute-start.5 = (f32[3,128,768]{1,2,0:T(8,128)}, f32[3,128,768]{1,2,0:T(8,128)}, u32[]{:S(2)}, u32[]{:S(2)}) collective-permute-start(f32[3,128,768]{1,2,0:T(8,128)} %pad_maximum_fusion), channel_id=1, source_target_pairs={{0,4},{4,0},{1,5},{5,1},{2,6},{6,2},{3,7},{7,3},{8,12},{12,8},{9,1... | collective-permute-start | bytes 3538952 | tf_op jit(solution)/shard_map/ppermute | solution.py:33
  35.5 1.3 copy-start.1
  35.5 1.3 copy-start.3
  41.3 10.1 %collective-permute-start.7 = (f32[1,128,768]{1,2,0:T(8,128)S(1)}, f32[1,128,768]{1,2,0:T(8,128)S(1)}, u32[]{:S(2)}, u32[]{:S(2)}) collective-permute-start(f32[1,128,768]{1,2,0:T(8,128)S(1)} %convert_subtract_fusion.1), channel_id=1, source_target_pairs={{1,0},{2,1},{3,2},{5,4},{6,5},{7,6},{9,8},{10,9},{11,10},{13,12},{... | collective-permute-start | bytes 1179656 | tf_op jit(solution)/shard_map/ppermute | solution.py:19
  43.4 11.9 %collective-permute-start.6 = (f32[1,128,768]{1,2,0:T(8,128)S(1)}, f32[1,128,768]{1,2,0:T(8,128)S(1)}, u32[]{:S(2)}, u32[]{:S(2)}) collective-permute-start(f32[1,128,768]{1,2,0:T(8,128)S(1)} %convert_subtract_fusion.1), channel_id=1, source_target_pairs={{0,1},{1,2},{2,3},{4,5},{5,6},{6,7},{8,9},{9,10},{10,11},{12,13},{... | collective-permute-start | bytes 1179656 | tf_op jit(solution)/shard_map/ppermute | solution.py:17
  56.4 4.2 %collective-permute-start.8 = (f32[3,128,768]{1,2,0:T(8,128)}, f32[3,128,768]{1,2,0:T(8,128)S(1)}, u32[]{:S(2)}, u32[]{:S(2)}) collective-permute-start(f32[3,128,768]{1,2,0:T(8,128)} %pad_maximum_fusion.1), channel_id=1, source_target_pairs={{0,4},{4,0},{1,5},{5,1},{2,6},{6,2},{3,7},{7,3},{8,12},{12,8},{9,1... | collective-permute-start | bytes 3538952 | tf_op jit(solution)/shard_map/ppermute | solution.py:33
  67.4 10.0 %collective-permute-start.10 = (f32[1,128,768]{1,2,0:T(8,128)S(1)}, f32[1,128,768]{1,2,0:T(8,128)S(1)}, u32[]{:S(2)}, u32[]{:S(2)}) collective-permute-start(f32[1,128,768]{1,2,0:T(8,128)S(1)} %add_multiply_fusion), channel_id=1, source_target_pairs={{1,0},{2,1},{3,2},{5,4},{6,5},{7,6},{9,8},{10,9},{11,10},{13,12},{... | collective-permute-start | bytes 1179656 | tf_op jit(solution)/shard_map/ppermute | solution.py:19
  69.3 11.9 %collective-permute-start.9 = (f32[1,128,768]{1,2,0:T(8,128)S(1)}, f32[1,128,768]{1,2,0:T(8,128)S(1)}, u32[]{:S(2)}, u32[]{:S(2)}) collective-permute-start(f32[1,128,768]{1,2,0:T(8,128)S(1)} %add_multiply_fusion), channel_id=1, source_target_pairs={{0,1},{1,2},{2,3},{4,5},{5,6},{6,7},{8,9},{9,10},{10,11},{12,13},{... | collective-permute-start | bytes 1179656 | tf_op jit(solution)/shard_map/ppermute | solution.py:17
  81.3 4.1 %collective-permute-start.11 = (f32[3,128,768]{1,2,0:T(8,128)S(1)}, f32[3,128,768]{1,2,0:T(8,128)S(1)}, u32[]{:S(2)}, u32[]{:S(2)}) collective-permute-start(f32[3,128,768]{1,2,0:T(8,128)S(1)} %pad_maximum_fusion.2), channel_id=1, source_target_pairs={{0,4},{4,0},{1,5},{5,1},{2,6},{6,2},{3,7},{7,3},{8,12},{12,8},{9,1... | collective-permute-start | bytes 3538952 | tf_op jit(solution)/shard_map/ppermute | solution.py:33
  88.4 10.0 %collective-permute-start.13 = (f32[1,128,768]{1,2,0:T(8,128)S(1)}, f32[1,128,768]{1,2,0:T(8,128)S(1)}, u32[]{:S(2)}, u32[]{:S(2)}) collective-permute-start(f32[1,128,768]{1,2,0:T(8,128)S(1)} %bitcast.713), channel_id=1, source_target_pairs={{1,0},{2,1},{3,2},{5,4},{6,5},{7,6},{9,8},{10,9},{11,10},{13,12},{... | collective-permute-start | bytes 1179656 | tf_op jit(solution)/shard_map/ppermute | solution.py:19
  90.3 11.9 %collective-permute-start.12 = (f32[1,128,768]{1,2,0:T(8,128)S(1)}, f32[1,128,768]{1,2,0:T(8,128)S(1)}, u32[]{:S(2)}, u32[]{:S(2)}) collective-permute-start(f32[1,128,768]{1,2,0:T(8,128)S(1)} %bitcast.714), channel_id=1, source_target_pairs={{0,1},{1,2},{2,3},{4,5},{5,6},{6,7},{8,9},{9,10},{10,11},{12,13},{... | collective-permute-start | bytes 1179656 | tf_op jit(solution)/shard_map/ppermute | solution.py:17
  102.3 4.0 %collective-permute-start.14 = (f32[3,128,768]{1,2,0:T(8,128)S(1)}, f32[3,128,768]{1,2,0:T(8,128)S(1)}, u32[]{:S(2)}, u32[]{:S(2)}) collective-permute-start(f32[3,128,768]{1,2,0:T(8,128)S(1)} %pad_maximum_fusion.3), channel_id=1, source_target_pairs={{0,4},{4,0},{1,5},{5,1},{2,6},{6,2},{3,7},{7,3},{8,12},{12,8},{9,1... | collective-permute-start | bytes 3538952 | tf_op jit(solution)/shard_map/ppermute | solution.py:33
  109.5 10.0 %collective-permute-start.16 = (f32[1,128,768]{1,2,0:T(8,128)S(1)}, f32[1,128,768]{1,2,0:T(8,128)S(1)}, u32[]{:S(2)}, u32[]{:S(2)}) collective-permute-start(f32[1,128,768]{1,2,0:T(8,128)S(1)} %convert_subtract_fusion), channel_id=1, source_target_pairs={{1,0},{2,1},{3,2},{5,4},{6,5},{7,6},{9,8},{10,9},{11,10},{13,12},{... | collective-permute-start | bytes 1179656 | tf_op jit(solution)/shard_map/ppermute | solution.py:19
  111.4 11.9 %collective-permute-start.15 = (f32[1,128,768]{1,2,0:T(8,128)S(1)}, f32[1,128,768]{1,2,0:T(8,128)S(1)}, u32[]{:S(2)}, u32[]{:S(2)}) collective-permute-start(f32[1,128,768]{1,2,0:T(8,128)S(1)} %convert_subtract_fusion), channel_id=1, source_target_pairs={{0,1},{1,2},{2,3},{4,5},{5,6},{6,7},{8,9},{9,10},{10,11},{12,13},{... | collective-permute-start | bytes 1179656 | tf_op jit(solution)/shard_map/ppermute | solution.py:17
  123.4 4.0 %collective-permute-start.17 = (f32[3,128,768]{1,2,0:T(8,128)S(1)}, f32[3,128,768]{1,2,0:T(8,128)S(1)}, u32[]{:S(2)}, u32[]{:S(2)}) collective-permute-start(f32[3,128,768]{1,2,0:T(8,128)S(1)} %pad_maximum_fusion.4), channel_id=1, source_target_pairs={{0,4},{4,0},{1,5},{5,1},{2,6},{6,2},{3,7},{7,3},{8,12},{12,8},{9,1... | collective-permute-start | bytes 3538952 | tf_op jit(solution)/shard_map/ppermute | solution.py:33
where the time goes:
time: 136 us; the launch traced here: 135 us
  waiting for transfers between devices  71.1 us (52%)
  starting transfers between devices  29.8 us (22%)
  matrix products  21.9 us (16%)
  other arithmetic  7.4 us (5%)
  local copies, waits for them, and re-layouts  4.11 us (3%)
    ppermute x6, waiting for transfers between devices, padded(): lax.ppermute(head, axis, [((i + 1) % count, i) for i in range(ends)])  35.6 us
    ppermute x6, waiting for transfers between devices, padded(): lax.ppermute(tail, axis, [(i, (i + 1) % count) for i in range(ends)])  23.1 us
    dot_general x42, matrix products, window_product(): lax.dot_general(left[:, slot], nearby[:, slot, :, source], (((1, 2), (0,...  16.5 us
    ppermute x6, waiting for transfers between devices, swapped(): return lax.ppermute(block, axis, route)  12.4 us
    ppermute x6, starting transfers between devices, padded(): lax.ppermute(head, axis, [((i + 1) % count, i) for i in range(ends)])  12 us
    ppermute x6, starting transfers between devices, swapped(): return lax.ppermute(block, axis, route)  9.62 us
    ppermute x6, starting transfers between devices, padded(): lax.ppermute(tail, axis, [(i, (i + 1) % count) for i in range(ends)])  8.15 us
    dot_general x14, matrix products, window_cross(): lax.dot_general(mines[slot], near_image[:, slot, :, source], (((0, 1), (0...  5.41 us
  transfers between devices with their start and end apart: 18, of which 18 were waited for; matrix products, arithmetic and copies ran while one was open for 2% of the time, Pallas kernels for 0%

commit v1 on v0

v1 whole, which is shorter than its diff:
```python
import jax
import jax.numpy as jnp
from jax import lax
from jax.experimental import pallas as pl
from jax.experimental.pallas import tpu as pltpu
from jax.sharding import PartitionSpec as P

ITERS = 2
BF = jnp.bfloat16
F32 = jnp.float32


def halves_of(value):
    high = value.astype(BF)
    low = (value - high.astype(F32)).astype(BF)
    return high, low


def product(left, right, dims):
    (lh, ll), (rh, rl) = left, right

    def dot(a, b):
        return lax.dot_general(a, b, (dims, ((), ())), preferred_element_type=F32)

    return dot(lh, rh) + (dot(lh, rl) + dot(ll, rh))


def nn(left, right):
    return product(left, right, ((1,), (0,)))


def tn(left, right):
    return product(left, right, ((0,), (0,)))


def ordered(side, own, other):
    return jnp.where(side == 0, own, other), jnp.where(side == 0, other, own)


def near(place, own, other):
    side, blk, last = place
    below, above = ordered(side, own, other)
    return jnp.where(blk > 0, below, 0.0), jnp.where(blk < last, above, 0.0)


def block_diag(top, bottom):
    zero = jnp.zeros_like(top)
    return jnp.concatenate(
        [jnp.concatenate([top, zero], axis=1), jnp.concatenate([zero, bottom], axis=1)], axis=0
    )


def place_of(ref):
    return ref[0], ref[1], ref[2]


def wide_row(side, own, other, rows):
    top, bottom = ordered(side, own, other)
    return [block_diag(top[:, e * rows:(e + 1) * rows], bottom[:, e * rows:(e + 1) * rows]) for e in range(3)]


def delta_column(s_row, s_below, s_above, z_row, z_below, z_above, width):
    s0, s1, s2 = [halves_of(v) for v in s_row]
    sb, sa = halves_of(s_below), halves_of(s_above)
    z0, z1, z2 = [halves_of(v) for v in z_row]
    zb0, zb1 = [halves_of(v) for v in z_below]
    za0, za1 = [halves_of(v) for v in z_above]
    i0 = halves_of(nn(sb, zb1) + tn(s0, z1))
    i1 = halves_of(nn(s0, zb1) + nn(s1, z1) + nn(s2, za0))
    i2 = halves_of(tn(s2, z1) + nn(sa, za0))
    d0 = -(tn(zb0, i0) + tn(z0, i1))
    row_ids = lax.broadcasted_iota(jnp.int32, (width, width), 0)
    col_ids = lax.broadcasted_iota(jnp.int32, (width, width), 1)
    eye = (row_ids == col_ids).astype(F32)
    d1 = eye - (tn(zb1, i0) + tn(z1, i1) + tn(za0, i2))
    d2 = -(tn(z2, i1) + tn(za1, i2))
    return d0, d1, d2


def write_delta(side, deltas, col_ref, pay_ref, width):
    for e in range(3):
        col_ref[e * width:(e + 1) * width, :] = deltas[e]
    for e in range(2):
        pay_ref[e * width:(e + 1) * width, :] = jnp.where(side == 0, deltas[e + 1], deltas[e])


def start_kernel(place, s_own, s_oth, h_own, h_oth, pay_ref):
    side = place[0]
    rows = s_own.shape[0]
    width = 2 * rows
    top, bottom = ordered(side, s_own[:, width:2 * width], s_oth[:, width:2 * width])
    pay_ref[:rows, :width] = top
    pay_ref[rows:, :width] = bottom
    pick = lambda ref: jnp.where(side == 0, ref[:, rows:3 * rows], ref[:, :2 * rows])
    top, bottom = ordered(side, pick(h_own), pick(h_oth))
    pay_ref[:rows, width:] = top
    pay_ref[rows:, width:] = bottom


def first_delta_kernel(place, s_own, s_oth, h_own, h_oth, r_own, r_oth, col_ref, pay_ref):
    where = place_of(place)
    side = where[0]
    rows = s_own.shape[0]
    width = 2 * rows
    s_all = jnp.concatenate(ordered(side, s_own[...], s_oth[...]), axis=0)
    s_row = [s_all[:, e * width:(e + 1) * width] for e in range(3)]
    z_row = wide_row(side, h_own[...], h_oth[...], rows)
    below, above = near(where, r_own[...], r_oth[...])

    def split(part):
        cells = part[:, width:]
        return [block_diag(cells[:rows, e * rows:(e + 1) * rows], cells[rows:, e * rows:(e + 1) * rows]) for e in range(2)]

    deltas = delta_column(s_row, below[:, :width], above[:, :width], z_row, split(below), split(above), width)
    write_delta(side, deltas, col_ref, pay_ref, width)


def next_delta_kernel(place, s_own, s_oth, s_rown, s_roth, z_ref, r_own, r_oth, col_ref, pay_ref):
    where = place_of(place)
    side = where[0]
    rows = s_own.shape[0]
    width = 2 * rows
    s_all = jnp.concatenate(ordered(side, s_own[...], s_oth[...]), axis=0)
    s_row = [s_all[:, e * width:(e + 1) * width] for e in range(3)]
    z_row = [z_ref[:, e * width:(e + 1) * width] for e in range(3)]
    s_below, s_above = near(where, s_rown[:, :width], s_roth[:, :width])
    below, above = near(where, r_own[...], r_oth[...])
    split = lambda part: [part[:, :width], part[:, width:]]
    deltas = delta_column(s_row, s_below, s_above, z_row, split(below), split(above), width)
    write_delta(side, deltas, col_ref, pay_ref, width)


def factor_rows(z_row, col_ref, below, above, width):
    z0, z1, z2 = [halves_of(v) for v in z_row]
    d = [halves_of(col_ref[e * width:(e + 1) * width, :]) for e in range(3)]
    b0, b1 = halves_of(below[:width]), halves_of(below[width:])
    a0, a1 = halves_of(above[:width]), halves_of(above[width:])

    def apply(x0, x1, x2):
        return (
            nn(x0, b0) + nn(x1, b1),
            nn(x0, d[0]) + nn(x1, d[1]) + nn(x2, d[2]),
            nn(x1, a0) + nn(x2, a1),
        )

    first = apply(z0, z1, z2)
    second = apply(*[halves_of(v) for v in first])
    return [z_row[e] + 0.5 * first[e] + 0.375 * second[e] for e in range(3)]


def kept(values, pattern, half, rows):
    count = pattern.shape[0]
    tile = rows // count
    bands = []
    for i in range(count):
        cells = []
        for q in range(6 * count):
            flag = jnp.logical_or(pattern[i, q] == 1, (2 + half) * count + i == q)
            cell = values[i * tile:(i + 1) * tile, q * tile:(q + 1) * tile]
            cells.append(jnp.where(flag, 1.0, 0.0) * cell)
        bands.append(jnp.concatenate(cells, axis=1))
    return bands[0] if count == 1 else jnp.concatenate(bands, axis=0)


def first_factor_kernel(place, pat_own, pat_oth, h_own, h_oth, col_ref, r_own, r_oth, z_ref, pay_ref):
    where = place_of(place)
    side = where[0]
    rows = h_own.shape[0]
    width = 2 * rows
    z_row = wide_row(side, h_own[...], h_oth[...], rows)
    below, above = near(where, r_own[...], r_oth[...])
    full = jnp.concatenate(factor_rows(z_row, col_ref, below, above, width), axis=1)
    own_rows = jnp.where(side == 0, full[:rows], full[rows:])
    oth_rows = jnp.where(side == 0, full[rows:], full[:rows])
    own_rows = kept(own_rows, pat_own, side, rows)
    oth_rows = kept(oth_rows, pat_oth, 1 - side, rows)
    top, bottom = ordered(side, own_rows, oth_rows)
    z_ref[:rows, :] = top
    z_ref[rows:, :] = bottom
    pay_ref[:rows, :] = jnp.where(side == 0, top[:, width:], top[:, :2 * width])
    pay_ref[rows:, :] = jnp.where(side == 0, bottom[:, width:], bottom[:, :2 * width])


def last_factor_kernel(place, pat_own, z_ref, col_ref, r_own, r_oth, out_ref):
    where = place_of(place)
    side = where[0]
    rows = out_ref.shape[0]
    width = 2 * rows
    mine = jnp.where(side == 0, z_ref[:rows, :], z_ref[rows:, :])
    z_row = [mine[:, e * width:(e + 1) * width] for e in range(3)]
    below, above = near(where, r_own[...], r_oth[...])
    full = jnp.concatenate(factor_rows(z_row, col_ref, below, above, width), axis=1)
    out_ref[...] = kept(full, pat_own, side, rows)


def call(kernel, outs, scalars, arrays):
    smem = pl.BlockSpec(memory_space=pltpu.SMEM)
    vmem = pl.BlockSpec(memory_space=pltpu.VMEM)
    shapes = [jax.ShapeDtypeStruct(s, F32) for s in outs]
    many = len(shapes) > 1
    return pl.pallas_call(
        kernel,
        out_shape=shapes if many else shapes[0],
        in_specs=[smem] * len(scalars) + [vmem] * len(arrays),
        out_specs=[vmem] * len(shapes) if many else vmem,
    )(*scalars, *arrays)


def per_device(intersect, half_factors, z_pattern):
    rows = intersect.shape[0]
    width = 2 * rows
    count = lax.axis_size("blk")
    side = lax.axis_index("side")
    place = jnp.stack([side, lax.axis_index("blk"), jnp.int32(count - 1)]).astype(jnp.int32)
    last = count - 1
    cycle = [(i, i + 1) for i in range(last)] + [(last, count + last)]
    cycle += [(count + i + 1, count + i) for i in range(last)] + [(count, 0)]

    def swap(value):
        return lax.ppermute(value, "side", [(0, 1), (1, 0)])

    def exchange(payload):
        got = lax.ppermute(payload, ("side", "blk"), cycle)
        return got, swap(got)

    s_oth, h_oth, p_oth = swap(intersect), swap(half_factors), swap(z_pattern)
    inputs = [intersect, s_oth, half_factors, h_oth]
    payload = call(start_kernel, [(width, 2 * width)], [place], inputs)
    near_in = exchange(payload)
    column, payload = call(first_delta_kernel, [(3 * width, width), (2 * width, width)], [place], inputs + list(near_in))
    near_delta = exchange(payload)
    for step in range(ITERS - 1):
        if step == 0:
            factor, payload = call(
                first_factor_kernel, [(width, 3 * width), (width, 2 * width)], [place, z_pattern, p_oth],
                [half_factors, h_oth, column, *near_delta])
        near_factor = exchange(payload)
        column, payload = call(
            next_delta_kernel, [(3 * width, width), (2 * width, width)], [place],
            [intersect, s_oth, *near_in, factor, *near_factor])
        near_delta = exchange(payload)
    return call(last_factor_kernel, [(rows, 3 * width)], [place, z_pattern], [factor, column, *near_delta])


def solution(mesh):
    spec = P(("pair", "side", "blk"), None)
    return jax.shard_map(
        per_device,
        mesh=mesh,
        in_specs=(spec, spec, spec),
        out_specs=spec,
        check_vma=False,
    )
```

time: 136 us -> 71.9 us (0.53)
  waiting for transfers between devices: 71.1 us -> 33.1 us
  matrix products: 21.9 us -> 0 us
  Pallas kernels: 0 us -> 18.9 us
  starting transfers between devices: 29.8 us -> 14 us
  other arithmetic: 7.4 us -> 0.61 us
    ppermute x18 -> x11, waiting for transfers between devices: 71.1 us -> 33.1 us  [the longest x4 25.8 us: exchange(): got = lax.ppermute(payload, ('side', 'blk'), cycle)]
    dot_general x56 -> x0, matrix products: 21.9 us -> none  [the longest x42 16.5 us: window_product(): lax.dot_general(left[:, slot], nearby[:, slot, :, source], (((1, 2), (0,...]
    pallas_call x0 -> x5, Pallas kernels: none -> 18.9 us  [call(): pl.pallas_call(kernel, out_shape=shapes if many else shapes[0], in_specs=...]
    ppermute x18 -> x11, starting transfers between devices: 29.8 us -> 14 us  [the longest x7 13.4 us: swap(): return lax.ppermute(value, 'side', [(0, 1), (1, 0)])]
    unnamed x15 -> x24, local copies, waits for them, and re-layouts: 1.86 us -> 4.6 us
    concatenate x6 -> x0, other arithmetic: 2.55 us -> none  [padded(): jnp.concatenate([lax.ppermute(tail, axis, [(i, (i + 1) % count) for i in...]
    select_n x6 -> x0, other arithmetic: 2.2 us -> none  [neighbours(): jnp.where(side == 0, local, other)]
    mul x9 -> x0, local copies, waits for them, and re-layouts: 1.8 us -> none  [the longest x5 1.57 us: per_device(): factor = keep * (factor + 0.5 * first + 0.375 * second)]
  transfers between devices with their start and end apart: 18 -> 11, of which waited for: 18 -> 9; matrix products, arithmetic and copies ran while one was open for 2% -> 1% of each run, Pallas kernels for 0% -> 0%
where the time goes in v1:
time: 71.9 us; the launch traced here: 71.2 us
  waiting for transfers between devices  33.1 us (46%)
  Pallas kernels  18.9 us (26%)
  starting transfers between devices  14 us (19%)
  local copies, waits for them, and re-layouts  4.6 us (6%)
    ppermute x4, waiting for transfers between devices, exchange(): got = lax.ppermute(payload, ('side', 'blk'), cycle)  25.8 us
    pallas_call x5, Pallas kernels, call(): pl.pallas_call(kernel, out_shape=shapes if many else shapes[0], in_specs=...  18.9 us
    ppermute x7, starting transfers between devices, swap(): return lax.ppermute(value, 'side', [(0, 1), (1, 0)])  13.4 us
    ppermute x7, waiting for transfers between devices, swap(): return lax.ppermute(value, 'side', [(0, 1), (1, 0)])  7.31 us
    unnamed x24, local copies, waits for them, and re-layouts  4.6 us
  transfers between devices with their start and end apart: 11, of which 9 were waited for; matrix products, arithmetic and copies ran while one was open for 1% of the time, Pallas kernels for 0%

profile of v1, /device:TPU:29, one launch (start us, length us, event | category | flops | bytes accessed | tf_op | source)
XLA Modules:
  0.0 71.2 jit_solution(12015608473366159742)
XLA Ops:
  0.0 0.7 collective-permute-start.2
  1.3 1.2 %collective-permute-done.1.h_oth = f32[128,384]{1,0:T(8,128)S(1)} collective-permute-done((f32[128,384]{1,0:T(8,128)}, f32[128,384]{1,0:T(8,128)S(1)}, u32[]{:S(2)}, u32[]{:S(2)}) %collective-permute-start.1) | collective-permute-done | bytes 196640 | tf_op jit(solution)/shard_map/ppermute | solution.py:220
  2.5 0.7 copy-done.3
  3.2 0.7 %copy-done = f32[128,768]{1,0:T(8,128)} copy-done((f32[128,768]{1,0:T(8,128)}, f32[128,768]{1,0:T(8,128)S(1)}, u32[]{:S(2)}) %copy-start) | copy-done | bytes 393240
  4.0 2.1 %shard_map.37 = f32[256,512]{1,0:T(8,128)} custom-call(s32[3]{0:T(128)} %pad_add_fusion.place, f32[128,768]{1,0:T(8,128)} %s_own.5, f32[128,768]{1,0:T(8,128)} %copy-done, f32[128,384]{1,0:T(8,128)} %h_own.5, f32[128,384]{1,0:T(8,128)} %copy-done.3), custom_call_target="tpu_custom_call" | custom-call | tf_op jit(solution)/shard_map/pallas_call | solution.py:201
  6.2 6.4 %collective-permute-done.3.r_own.s_rown = f32[256,512]{1,0:T(8,128)S(1)} collective-permute-done((f32[256,512]{1,0:T(8,128)}, f32[256,512]{1,0:T(8,128)S(1)}, u32[]{:S(2)}, u32[]{:S(2)}) %collective-permute-start.3) | collective-permute-done | bytes 524320 | tf_op jit(solution)/shard_map/ppermute | solution.py:223
  12.7 3.2 %collective-permute-start.4 = (f32[256,512]{1,0:T(8,128)S(1)}, f32[256,512]{1,0:T(8,128)S(1)}, u32[]{:S(2)}, u32[]{:S(2)}) collective-permute-start(f32[256,512]{1,0:T(8,128)S(1)} %collective-permute-done.3.r_own.s_rown), channel_id=1, source_target_pairs={{0,4},{4,0},{1,5},{5,1},{2,6},{6,2},{3,7},{7,3},{8,12},{12,8},{9,1... | collective-permute-start | bytes 1572872 | tf_op jit(solution)/shard_map/ppermute | solution.py:220
  15.8 1.5 %collective-permute-done.4.r_oth.s_roth = f32[256,512]{1,0:T(8,128)S(1)} collective-permute-done((f32[256,512]{1,0:T(8,128)S(1)}, f32[256,512]{1,0:T(8,128)S(1)}, u32[]{:S(2)}, u32[]{:S(2)}) %collective-permute-start.4) | collective-permute-done | bytes 524320 | tf_op jit(solution)/shard_map/ppermute | solution.py:220
  17.3 0.8 %copy-done.2 = f32[256,512]{1,0:T(8,128)} copy-done((f32[256,512]{1,0:T(8,128)}, f32[256,512]{1,0:T(8,128)S(1)}, u32[]{:S(2)}) %copy-start.2) | copy-done | bytes 524312
  18.1 4.3 %shard_map.38 = (f32[768,256]{1,0:T(8,128)}, f32[512,256]{1,0:T(8,128)}) custom-call(s32[3]{0:T(128)} %pad_add_fusion.place, f32[128,768]{1,0:T(8,128)} %s_own.5, f32[128,768]{1,0:T(8,128)} %copy-done, f32[128,384]{1,0:T(8,128)} %h_own.5, f32[128,384]{1,0:T(8,128)} %copy-done.3, f32[256,512]{1,0:T(8,128)} %copy-done.1, f32[256,512]{1,0:T(8,128)} %copy-done.2), custom_call_target="tpu_custom_call" | custom-call | tf_op jit(solution)/shard_map/pallas_call | solution.py:201
  22.6 6.4 %collective-permute-done.5.r_own = f32[512,256]{1,0:T(8,128)S(1)} collective-permute-done((f32[512,256]{1,0:T(8,128)}, f32[512,256]{1,0:T(8,128)S(1)}, u32[]{:S(2)}, u32[]{:S(2)}) %collective-permute-start.5) | collective-permute-done | bytes 524320 | tf_op jit(solution)/shard_map/ppermute | solution.py:223
  29.0 3.2 %collective-permute-start.6 = (f32[512,256]{1,0:T(8,128)S(1)}, f32[512,256]{1,0:T(8,128)S(1)}, u32[]{:S(2)}, u32[]{:S(2)}) collective-permute-start(f32[512,256]{1,0:T(8,128)S(1)} %collective-permute-done.5.r_own), channel_id=1, source_target_pairs={{0,4},{4,0},{1,5},{5,1},{2,6},{6,2},{3,7},{7,3},{8,12},{12,8},{9,1... | collective-permute-start | bytes 1572872 | tf_op jit(solution)/shard_map/ppermute | solution.py:220
  32.3 1.5 %collective-permute-done.pat_oth = s32[1,6]{1,0:T(1,128)S(1)} collective-permute-done((s32[1,6]{1,0:T(1,128)S(1)}, s32[1,6]{1,0:T(1,128)S(1)}, u32[]{:S(2)}, u32[]{:S(2)}) %collective-permute-start) | collective-permute-done | bytes 56 | tf_op jit(solution)/shard_map/ppermute | solution.py:220
  34.5 4.4 %shard_map.39 = (f32[256,768]{1,0:T(8,128)}, f32[256,512]{1,0:T(8,128)}) custom-call(s32[3]{0:T(128)} %pad_add_fusion.place, s32[1,6]{1,0:T(1,128)} %pat_own.3, s32[1,6]{1,0:T(1,128)} %copy-done.11, f32[128,384]{1,0:T(8,128)} %h_own.5, f32[128,384]{1,0:T(8,128)} %copy-done.3, f32[768,256]{1,0:T(8,128)} %get-tuple-element.11.col_ref, f32[512,256]{1,0:T(8,128)} %copy-done.4, ...), custom_call_target="tpu_custom_call" | custom-call | tf_op jit(solution)/shard_map/pallas_call | solution.py:201
  39.0 6.4 %collective-permute-done.7.r_own = f32[256,512]{1,0:T(8,128)S(1)} collective-permute-done((f32[256,512]{1,0:T(8,128)}, f32[256,512]{1,0:T(8,128)S(1)}, u32[]{:S(2)}, u32[]{:S(2)}) %collective-permute-start.7) | collective-permute-done | bytes 524320 | tf_op jit(solution)/shard_map/ppermute | solution.py:223
  45.5 3.2 %collective-permute-start.8 = (f32[256,512]{1,0:T(8,128)S(1)}, f32[256,512]{1,0:T(8,128)S(1)}, u32[]{:S(2)}, u32[]{:S(2)}) collective-permute-start(f32[256,512]{1,0:T(8,128)S(1)} %collective-permute-done.7.r_own), channel_id=1, source_target_pairs={{0,4},{4,0},{1,5},{5,1},{2,6},{6,2},{3,7},{7,3},{8,12},{12,8},{9,1... | collective-permute-start | bytes 1572872 | tf_op jit(solution)/shard_map/ppermute | solution.py:220
  48.6 1.5 %collective-permute-done.8.r_oth = f32[256,512]{1,0:T(8,128)S(1)} collective-permute-done((f32[256,512]{1,0:T(8,128)S(1)}, f32[256,512]{1,0:T(8,128)S(1)}, u32[]{:S(2)}, u32[]{:S(2)}) %collective-permute-start.8) | collective-permute-done | bytes 524320 | tf_op jit(solution)/shard_map/ppermute | solution.py:220
  50.2 0.8 %copy-done.8 = f32[256,512]{1,0:T(8,128)} copy-done((f32[256,512]{1,0:T(8,128)}, f32[256,512]{1,0:T(8,128)S(1)}, u32[]{:S(2)}) %copy-start.8) | copy-done | bytes 524312
  51.0 4.8 %shard_map.40 = (f32[768,256]{1,0:T(8,128)}, f32[512,256]{1,0:T(8,128)}) custom-call(s32[3]{0:T(128)} %pad_add_fusion.place, f32[128,768]{1,0:T(8,128)} %s_own.5, f32[128,768]{1,0:T(8,128)} %copy-done, f32[256,512]{1,0:T(8,128)} %copy-done.1, f32[256,512]{1,0:T(8,128)} %copy-done.2, f32[256,768]{1,0:T(8,128)} %get-tuple-element.13.z_ref, ...), custom_call_target="tpu_custom_call" | custom-call | tf_op jit(solution)/shard_map/pallas_call | solution.py:201
  55.9 6.4 %collective-permute-done.9.r_own = f32[512,256]{1,0:T(8,128)S(1)} collective-permute-done((f32[512,256]{1,0:T(8,128)}, f32[512,256]{1,0:T(8,128)S(1)}, u32[]{:S(2)}, u32[]{:S(2)}) %collective-permute-start.9) | collective-permute-done | bytes 524320 | tf_op jit(solution)/shard_map/ppermute | solution.py:223
  62.3 3.2 %collective-permute-start.10 = (f32[512,256]{1,0:T(8,128)S(1)}, f32[512,256]{1,0:T(8,128)S(1)}, u32[]{:S(2)}, u32[]{:S(2)}) collective-permute-start(f32[512,256]{1,0:T(8,128)S(1)} %collective-permute-done.9.r_own), channel_id=1, source_target_pairs={{0,4},{4,0},{1,5},{5,1},{2,6},{6,2},{3,7},{7,3},{8,12},{12,8},{9,1... | collective-permute-start | bytes 1572872 | tf_op jit(solution)/shard_map/ppermute | solution.py:220
  65.5 1.5 %collective-permute-done.10.r_oth = f32[512,256]{1,0:T(8,128)S(1)} collective-permute-done((f32[512,256]{1,0:T(8,128)S(1)}, f32[512,256]{1,0:T(8,128)S(1)}, u32[]{:S(2)}, u32[]{:S(2)}) %collective-permute-start.10) | collective-permute-done | bytes 524320 | tf_op jit(solution)/shard_map/ppermute | solution.py:220
  67.0 0.8 %copy-done.9 = f32[512,256]{1,0:T(8,128)} copy-done((f32[512,256]{1,0:T(8,128)}, f32[512,256]{1,0:T(8,128)S(1)}, u32[]{:S(2)}) %copy-start.9) | copy-done | bytes 524312
  67.8 3.4 %shard_map.41 = f32[128,768]{1,0:T(8,128)} custom-call(s32[3]{0:T(128)} %pad_add_fusion.place, s32[1,6]{1,0:T(1,128)} %pat_own.3, f32[256,768]{1,0:T(8,128)} %get-tuple-element.13.z_ref, f32[768,256]{1,0:T(8,128)} %get-tuple-element.15.col_ref, f32[512,256]{1,0:T(8,128)} %copy-done.7, f32[512,256]{1,0:T(8,128)} %copy-done.9), custom_call_target="tpu_custom_call" | custom-call | tf_op jit(solution)/shard_map/pallas_call | solution.py:201
  (28 shorter events, 2.2 us)
Async XLA Ops:
  0.0 2.5 %collective-permute-start.2 = (f32[128,768]{1,0:T(8,128)}, f32[128,768]{1,0:T(8,128)S(1)}, u32[]{:S(2)}, u32[]{:S(2)}) collective-permute-start(f32[128,768]{1,0:T(8,128)} %s_own.5), channel_id=1, source_target_pairs={{0,4},{4,0},{1,5},{5,1},{2,6},{6,2},{3,7},{7,3},{8,12},{12,8},{9,1... | collective-permute-start | bytes 1179656 | tf_op jit(solution)/shard_map/ppermute | solution.py:220
  0.7 1.8 %collective-permute-start.1 = (f32[128,384]{1,0:T(8,128)}, f32[128,384]{1,0:T(8,128)S(1)}, u32[]{:S(2)}, u32[]{:S(2)}) collective-permute-start(f32[128,384]{1,0:T(8,128)} %h_own.5), channel_id=1, source_target_pairs={{0,4},{4,0},{1,5},{5,1},{2,6},{6,2},{3,7},{7,3},{8,12},{12,8},{9,1... | collective-permute-start | bytes 589832 | tf_op jit(solution)/shard_map/ppermute | solution.py:220
  2.5 0.7 copy-start.3
  3.2 0.7 %copy-start = (f32[128,768]{1,0:T(8,128)}, f32[128,768]{1,0:T(8,128)S(1)}, u32[]{:S(2)}) copy-start(f32[128,768]{1,0:T(8,128)S(1)} %collective-permute-done.2.s_oth) | copy-start | bytes 1179652
  6.0 6.6 %collective-permute-start.3 = (f32[256,512]{1,0:T(8,128)}, f32[256,512]{1,0:T(8,128)S(1)}, u32[]{:S(2)}, u32[]{:S(2)}) collective-permute-start(f32[256,512]{1,0:T(8,128)} %shard_map.37), channel_id=1, source_target_pairs={{0,1},{1,2},{2,3},{3,7},{5,4},{6,5},{7,6},{4,0},{8,9},{9,10},{10,1... | collective-permute-start | bytes 1572872 | tf_op jit(solution)/shard_map/ppermute | solution.py:223
  12.7 4.7 %copy-start.1 = (f32[256,512]{1,0:T(8,128)}, f32[256,512]{1,0:T(8,128)S(1)}, u32[]{:S(2)}) copy-start(f32[256,512]{1,0:T(8,128)S(1)} %collective-permute-done.3.r_own.s_rown) | copy-start | bytes 1572868
  12.7 4.7 %collective-permute-start.4 = (f32[256,512]{1,0:T(8,128)S(1)}, f32[256,512]{1,0:T(8,128)S(1)}, u32[]{:S(2)}, u32[]{:S(2)}) collective-permute-start(f32[256,512]{1,0:T(8,128)S(1)} %collective-permute-done.3.r_own.s_rown), channel_id=1, source_target_pairs={{0,4},{4,0},{1,5},{5,1},{2,6},{6,2},{3,7},{7,3},{8,12},{12,8},{9,1... | collective-permute-start | bytes 1572872 | tf_op jit(solution)/shard_map/ppermute | solution.py:220
  17.3 0.8 %copy-start.2 = (f32[256,512]{1,0:T(8,128)}, f32[256,512]{1,0:T(8,128)S(1)}, u32[]{:S(2)}) copy-start(f32[256,512]{1,0:T(8,128)S(1)} %collective-permute-done.4.r_oth.s_roth) | copy-start | bytes 1572868
  22.4 9.8 %copy-start.10 = (s32[1,6]{1,0:T(1,128)S(1)}, s32[1,6]{1,0:T(1,128)}, u32[]{:S(2)}) copy-start(s32[1,6]{1,0:T(1,128)} %pat_own.3) | copy-start | bytes 76
  22.4 6.6 %collective-permute-start.5 = (f32[512,256]{1,0:T(8,128)}, f32[512,256]{1,0:T(8,128)S(1)}, u32[]{:S(2)}, u32[]{:S(2)}) collective-permute-start(f32[512,256]{1,0:T(8,128)} %get-tuple-element.12), channel_id=1, source_target_pairs={{0,1},{1,2},{2,3},{3,7},{5,4},{6,5},{7,6},{4,0},{8,9},{9,10},{10,1... | collective-permute-start | bytes 1572872 | tf_op jit(solution)/shard_map/ppermute | solution.py:223
  29.0 4.7 %copy-start.4 = (f32[512,256]{1,0:T(8,128)}, f32[512,256]{1,0:T(8,128)S(1)}, u32[]{:S(2)}) copy-start(f32[512,256]{1,0:T(8,128)S(1)} %collective-permute-done.5.r_own) | copy-start | bytes 1572868
  29.0 4.7 %collective-permute-start.6 = (f32[512,256]{1,0:T(8,128)S(1)}, f32[512,256]{1,0:T(8,128)S(1)}, u32[]{:S(2)}, u32[]{:S(2)}) collective-permute-start(f32[512,256]{1,0:T(8,128)S(1)} %collective-permute-done.5.r_own), channel_id=1, source_target_pairs={{0,4},{4,0},{1,5},{5,1},{2,6},{6,2},{3,7},{7,3},{8,12},{12,8},{9,1... | collective-permute-start | bytes 1572872 | tf_op jit(solution)/shard_map/ppermute | solution.py:220
  32.2 1.5 %collective-permute-start = (s32[1,6]{1,0:T(1,128)S(1)}, s32[1,6]{1,0:T(1,128)S(1)}, u32[]{:S(2)}, u32[]{:S(2)}) collective-permute-start(s32[1,6]{1,0:T(1,128)S(1)} %copy-done.10), channel_id=1, source_target_pairs={{0,4},{4,0},{1,5},{5,1},{2,6},{6,2},{3,7},{7,3},{8,12},{12,8},{9,1... | collective-permute-start | bytes 80 | tf_op jit(solution)/shard_map/ppermute | solution.py:220
  33.7 0.6 copy-start.11
  33.7 0.8 %copy-start.5 = (f32[512,256]{1,0:T(8,128)}, f32[512,256]{1,0:T(8,128)S(1)}, u32[]{:S(2)}) copy-start(f32[512,256]{1,0:T(8,128)S(1)} %collective-permute-done.6.r_oth) | copy-start | bytes 1572868
  38.9 6.6 %collective-permute-start.7 = (f32[256,512]{1,0:T(8,128)}, f32[256,512]{1,0:T(8,128)S(1)}, u32[]{:S(2)}, u32[]{:S(2)}) collective-permute-start(f32[256,512]{1,0:T(8,128)} %get-tuple-element.14), channel_id=1, source_target_pairs={{0,1},{1,2},{2,3},{3,7},{5,4},{6,5},{7,6},{4,0},{8,9},{9,10},{10,1... | collective-permute-start | bytes 1572872 | tf_op jit(solution)/shard_map/ppermute | solution.py:223
  45.5 4.7 %copy-start.6 = (f32[256,512]{1,0:T(8,128)}, f32[256,512]{1,0:T(8,128)S(1)}, u32[]{:S(2)}) copy-start(f32[256,512]{1,0:T(8,128)S(1)} %collective-permute-done.7.r_own) | copy-start | bytes 1572868
  45.5 4.7 %collective-permute-start.8 = (f32[256,512]{1,0:T(8,128)S(1)}, f32[256,512]{1,0:T(8,128)S(1)}, u32[]{:S(2)}, u32[]{:S(2)}) collective-permute-start(f32[256,512]{1,0:T(8,128)S(1)} %collective-permute-done.7.r_own), channel_id=1, source_target_pairs={{0,4},{4,0},{1,5},{5,1},{2,6},{6,2},{3,7},{7,3},{8,12},{12,8},{9,1... | collective-permute-start | bytes 1572872 | tf_op jit(solution)/shard_map/ppermute | solution.py:220
  50.2 0.8 %copy-start.8 = (f32[256,512]{1,0:T(8,128)}, f32[256,512]{1,0:T(8,128)S(1)}, u32[]{:S(2)}) copy-start(f32[256,512]{1,0:T(8,128)S(1)} %collective-permute-done.8.r_oth) | copy-start | bytes 1572868
  55.7 6.6 %collective-permute-start.9 = (f32[512,256]{1,0:T(8,128)}, f32[512,256]{1,0:T(8,128)S(1)}, u32[]{:S(2)}, u32[]{:S(2)}) collective-permute-start(f32[512,256]{1,0:T(8,128)} %get-tuple-element.16), channel_id=1, source_target_pairs={{0,1},{1,2},{2,3},{3,7},{5,4},{6,5},{7,6},{4,0},{8,9},{9,10},{10,1... | collective-permute-start | bytes 1572872 | tf_op jit(solution)/shard_map/ppermute | solution.py:223
  62.3 4.7 %copy-start.7 = (f32[512,256]{1,0:T(8,128)}, f32[512,256]{1,0:T(8,128)S(1)}, u32[]{:S(2)}) copy-start(f32[512,256]{1,0:T(8,128)S(1)} %collective-permute-done.9.r_own) | copy-start | bytes 1572868
  62.3 4.7 %collective-permute-start.10 = (f32[512,256]{1,0:T(8,128)S(1)}, f32[512,256]{1,0:T(8,128)S(1)}, u32[]{:S(2)}, u32[]{:S(2)}) collective-permute-start(f32[512,256]{1,0:T(8,128)S(1)} %collective-permute-done.9.r_own), channel_id=1, source_target_pairs={{0,4},{4,0},{1,5},{5,1},{2,6},{6,2},{3,7},{7,3},{8,12},{12,8},{9,1... | collective-permute-start | bytes 1572872 | tf_op jit(solution)/shard_map/ppermute | solution.py:220
  67.0 0.8 %copy-start.9 = (f32[512,256]{1,0:T(8,128)}, f32[512,256]{1,0:T(8,128)S(1)}, u32[]{:S(2)}) copy-start(f32[512,256]{1,0:T(8,128)S(1)} %collective-permute-done.10.r_oth) | copy-start | bytes 1572868

commit v2 on v1

v2 whole, which is shorter than its diff:
```python
import jax
import jax.numpy as jnp
from jax import lax
from jax.experimental import pallas as pl
from jax.experimental.pallas import tpu as pltpu
from jax.sharding import PartitionSpec as P


ITERS = 2
BF = jnp.bfloat16
F32 = jnp.float32


def halves_of(value):
    high = value.astype(BF)
    low = (value - high.astype(F32)).astype(BF)
    return high, low


def product(left, right, dims):
    (lh, ll), (rh, rl) = left, right

    def dot(a, b):
        return lax.dot_general(a, b, (dims, ((), ())), preferred_element_type=F32)

    return dot(lh, rh) + (dot(lh, rl) + dot(ll, rh))


def nn(left, right):
    return product(left, right, ((1,), (0,)))


def tn(left, right):
    return product(left, right, ((0,), (0,)))


def ordered(side, own, other):
    return jnp.where(side == 0, own, other), jnp.where(side == 0, other, own)


def block_diag(top, bottom):
    zero = jnp.zeros_like(top)
    return jnp.concatenate(
        [jnp.concatenate([top, zero], axis=1), jnp.concatenate([zero, bottom], axis=1)], axis=0
    )


def oriented(side, row, width):
    first, middle, final = [row[:, e * width:(e + 1) * width] for e in range(3)]
    near, far = ordered(side, first, final)
    return near, middle, far


def start_kernel(place, pattern, s_own, s_oth, h_own, h_oth, pay_ref):
    side = place[0]
    rows = s_own.shape[0]
    width = 2 * rows
    top, bottom = ordered(side, s_own[:, width:2 * width], s_oth[:, width:2 * width])
    pay_ref[:rows, :width] = top
    pay_ref[rows:, :width] = bottom
    top, bottom = ordered(side, h_own[...], h_oth[...])
    for part, at in ((top, 0), (bottom, rows)):
        _, middle, far = oriented(side, part, rows)
        pay_ref[at:at + rows, width:width + rows] = middle
        pay_ref[at:at + rows, width + rows:] = far


def image_local(s_row, z_mid, outs):
    near, middle, far = [halves_of(v) for v in s_row]
    z = halves_of(z_mid)
    outs[0][...] = tn(near, z)
    outs[1][...] = nn(middle, z)
    outs[2][...] = tn(far, z)


def first_local_kernel(place, s_own, s_oth, h_own, h_oth, sn, sm, sf, zn, zm, zf, tn_, tm, tf):
    side = place[0]
    rows = s_own.shape[0]
    width = 2 * rows
    s_all = jnp.concatenate(ordered(side, s_own[...], s_oth[...]), axis=0)
    s_row = oriented(side, s_all, width)
    top, bottom = ordered(side, h_own[...], h_oth[...])
    z_row = [block_diag(a, b) for a, b in zip(oriented(side, top, rows), oriented(side, bottom, rows))]
    for ref, v in zip((sn, sm, sf, zn, zm, zf), [*s_row, *z_row]):
        ref[...] = v
    image_local(s_row, z_row[1], (tn_, tm, tf))


def next_local_kernel(place, sn, sm, sf, zm, tn_, tm, tf):
    image_local((sn[...], sm[...], sf[...]), zm[...], (tn_, tm, tf))


def factor_parts(got_ref, keep, split):
    got = jnp.where(keep == 1, got_ref[...], 0.0)
    width = got.shape[0]
    if not split:
        return got[:, :width], got[:, width:]
    rows = width // 2
    cells = got[:, width:]
    return [block_diag(cells[:rows, e * rows:(e + 1) * rows], cells[rows:, e * rows:(e + 1) * rows]) for e in range(2)]


def overlap_part(got_ref, keep, width):
    return halves_of(jnp.where(keep == 1, got_ref[:, :width], 0.0))


def near_image_kernel(split):
    def kernel(place, s_got, z_got, sn, t_near, t_mid, mid_ref, e_near, e_mid):
        width = t_near.shape[0]
        diag, off = [halves_of(v) for v in factor_parts(z_got, place[1], split)]
        image_near = halves_of(nn(overlap_part(s_got, place[1], width), off) + t_near[...])
        mid_ref[...] = t_mid[...] + nn(halves_of(sn[...]), off)
        e_near[...] = tn(diag, image_near)
        e_mid[...] = tn(off, image_near)

    return kernel


def far_image_kernel(split):
    def kernel(place, s_got, z_got, sf, zm, zf, t_far, mid_part, e_mid, mid_ref, pay_ref):
        width = t_far.shape[0]
        diag, off = [halves_of(v) for v in factor_parts(z_got, place[2], split)]
        middle = mid_part[...] + nn(halves_of(sf[...]), off)
        mid_ref[...] = middle
        middle = halves_of(middle)
        image_far = halves_of(nn(overlap_part(s_got, place[2], width), off) + t_far[...])
        row_ids = lax.broadcasted_iota(jnp.int32, (width, width), 0)
        col_ids = lax.broadcasted_iota(jnp.int32, (width, width), 1)
        eye = (row_ids == col_ids).astype(F32)
        pay_ref[:width] = eye - (e_mid[...] + tn(halves_of(zm[...]), middle) + tn(off, image_far))
        pay_ref[width:] = -(tn(halves_of(zf[...]), middle) + tn(diag, image_far))

    return kernel


def own_rows(ref, side, rows):
    if ref.shape[0] == rows:
        return ref[...]
    return jnp.where(side == 0, ref[:rows, :], ref[rows:, :])


def mid_first_kernel(place, zn, zm, zf, e_near, mid, pay, d_near, first_ref, part_ref):
    side = place[0]
    width = zn.shape[0]
    rows = first_ref.shape[0]
    d_new = -(e_near[...] + tn(halves_of(zn[...]), halves_of(mid[...])))
    d_near[...] = d_new
    d_mid = halves_of(pay[:width])
    first = nn(halves_of(own_rows(zn, side, rows)), halves_of(d_new))
    first += nn(halves_of(own_rows(zm, side, rows)), d_mid)
    first += nn(halves_of(own_rows(zf, side, rows)), halves_of(pay[width:]))
    first_ref[...] = first
    part_ref[...] = nn(halves_of(first), d_mid)


def kept(values, pats, side, slot, rows):
    count = pats[0].shape[0]
    tile = rows // count
    both = values.shape[0] != rows
    bands = []
    for f in range(2 if both else 1):
        half = f if both else side
        for i in range(count):
            cells = []
            for q in range(2 * count):
                at = slot * 2 * count + q
                bit = jnp.where(side == f, pats[0][i, at], pats[1][i, at]) if both else pats[0][i, at]
                flag = jnp.logical_or(bit == 1, (2 + half) * count + i == at)
                top = (f * count + i) * tile
                cell = values[top:top + tile, q * tile:(q + 1) * tile]
                cells.append(jnp.where(flag, 1.0, 0.0) * cell)
            bands.append(jnp.concatenate(cells, axis=1))
    return jnp.concatenate(bands, axis=0) if len(bands) > 1 else bands[0]


def side_products(got, keep, z_side, z_mid, first, width):
    got = jnp.where(keep == 1, got, 0.0)
    diag, off = halves_of(got[:width]), halves_of(got[width:])
    outer = nn(halves_of(z_side), diag) + nn(halves_of(z_mid), off)
    split = halves_of(outer)
    second = nn(split, diag) + nn(halves_of(first), off)
    return outer, split, second


def near_factor_kernel(place, *refs):
    pats, (got, zn, zm, first, part, d_near, new_ref, part_ref) = refs[:-8], refs[-8:]
    side = place[0]
    rows = zn.shape[0] // 2
    size = first.shape[0]
    z = own_rows(zn, side, size)
    outer, split, second = side_products(got[...], place[1], z, own_rows(zm, side, size), first[...], 2 * rows)
    part_ref[...] = part[...] + nn(split, halves_of(d_near[...]))
    new_ref[...] = kept(z + 0.5 * outer + 0.375 * second, pats, side, 2 * side, rows)


def far_blocks(place, pats, got, zm, zf, first, part, pay):
    side = place[0]
    width = zm.shape[0]
    rows = width // 2
    size = first.shape[0]
    z, mid = own_rows(zf, side, size), own_rows(zm, side, size)
    outer, split, second = side_products(got[...], place[2], z, mid, first[...], width)
    second_mid = part[...] + nn(split, halves_of(pay[width:]))
    far = kept(z + 0.5 * outer + 0.375 * second, pats, side, 2 - 2 * side, rows)
    return kept(mid + 0.5 * first[...] + 0.375 * second_mid, pats, side, 1, rows), far


def far_factor_kernel(place, pat_own, pat_oth, got, zm, zf, first, part, pay, pay_ref):
    width = zm.shape[0]
    middle, far = far_blocks(place, (pat_own, pat_oth), got, zm, zf, first, part, pay)
    pay_ref[:, :width] = middle
    pay_ref[:, width:] = far


def last_factor_kernel(place, pat_own, got, zm, zf, first, part, pay, near, out_ref):
    side = place[0]
    width = zm.shape[0]
    middle, far = far_blocks(place, (pat_own,), got, zm, zf, first, part, pay)
    low, high = ordered(side, near[...], far)
    out_ref[:, :width] = low
    out_ref[:, width:2 * width] = middle
    out_ref[:, 2 * width:] = high


def call(kernel, outs, scalars, arrays, flops=10**9):
    smem = pl.BlockSpec(memory_space=pltpu.SMEM)
    vmem = pl.BlockSpec(memory_space=pltpu.VMEM)
    shapes = [jax.ShapeDtypeStruct(s, F32) for s in outs]
    many = len(shapes) > 1
    return pl.pallas_call(
        kernel,
        out_shape=shapes if many else shapes[0],
        in_specs=[smem] * len(scalars) + [vmem] * len(arrays),
        out_specs=[vmem] * len(shapes) if many else vmem,
        cost_estimate=pl.CostEstimate(flops=flops, bytes_accessed=0, transcendentals=0),
        compiler_params=pltpu.CompilerParams(vmem_limit_bytes=16 * 2**20),
    )(*scalars, *arrays)


def per_device(intersect, half_factors, z_pattern):
    rows = intersect.shape[0]
    width = 2 * rows
    square = (width, width)
    count = lax.axis_size("blk")
    last = count - 1
    side = lax.axis_index("side")
    blk = lax.axis_index("blk")
    inner = jnp.stack([blk > 0, blk < last])
    place = jnp.stack([side, jnp.where(side == 0, inner[0], inner[1]), jnp.where(side == 0, inner[1], inner[0])])
    place = place.astype(jnp.int32)
    cycle = [(i, i + 1) for i in range(last)] + [(last, count + last)]
    cycle += [(count + i + 1, count + i) for i in range(last)] + [(count, 0)]

    def swap(value):
        return lax.ppermute(value, "side", [(0, 1), (1, 0)])

    def exchange(payload):
        got = lax.ppermute(payload, ("side", "blk"), cycle)
        return got, swap(got)

    s_oth, h_oth, p_oth = swap(intersect), swap(half_factors), swap(z_pattern)
    inputs = [intersect, s_oth, half_factors, h_oth]
    payload = call(start_kernel, [(width, 2 * width)], [place, p_oth], inputs)
    s_near, s_far = exchange(payload)
    z_near, z_far = s_near, s_far
    sn, sm, sf, zn, zm, zf, t_near, t_mid, t_far = call(first_local_kernel, [square] * 9, [place], inputs)
    for step in range(ITERS):
        final = step == ITERS - 1
        if step > 0:
            z_near, z_far = exchange(payload)
            t_near, t_mid, t_far = call(next_local_kernel, [square] * 3, [place], [sn, sm, sf, zm])
        mid, e_near, e_mid = call(
            near_image_kernel(step == 0), [square] * 3, [place], [s_near, z_near, sn, t_near, t_mid])
        mid, delta = call(
            far_image_kernel(step == 0), [square, (2 * width, width)], [place],
            [s_far, z_far, sf, zm, zf, t_far, mid, e_mid])
        d_own, d_oth = exchange(delta)
        band = (rows if final else width, width)
        pats = [z_pattern] if final else [z_pattern, p_oth]
        d_near, first, part = call(
            mid_first_kernel, [square, band, band], [place], [zn, zm, zf, e_near, mid, delta])
        near, part = call(near_factor_kernel, [band, band], [place] + pats, [d_own, zn, zm, first, part, d_near])
        rest = [d_oth, zm, zf, first, part, delta]
        if final:
            return call(last_factor_kernel, [(rows, 3 * width)], [place] + pats, rest + [near])
        payload = call(far_factor_kernel, [(width, 2 * width)], [place] + pats, rest)
        zn, zm, zf = near, payload[:, :width], payload[:, width:]


def solution(mesh):
    spec = P(("pair", "side", "blk"), None)
    return jax.shard_map(
        per_device,
        mesh=mesh,
        in_specs=(spec, spec, spec),
        out_specs=spec,
        check_vma=False,
    )
```

time: 71.9 us -> 60.6 us (0.84)
  waiting for transfers between devices: 33.1 us -> 25.8 us
  local copies, waits for them, and re-layouts: 4.6 us -> 2.61 us
  Pallas kernels: 18.9 us -> 17.9 us
    ppermute x7, waiting for transfers between devices: 7.31 us -> 1.27 us  [swap(): return lax.ppermute(value, 'side', [(0, 1), (1, 0)])]
    unnamed x24 -> x8, local copies, waits for them, and re-layouts: 4.6 us -> 2.58 us
    ppermute x4, waiting for transfers between devices: 25.8 us -> 24.5 us  [exchange(): got = lax.ppermute(payload, ('side', 'blk'), cycle)]
    pallas_call x5 -> x13, Pallas kernels: 18.9 us -> 17.9 us  [call(): pl.pallas_call(kernel, out_shape=shapes if many else shapes[0], in_specs=...]
  transfers between devices with their start and end apart: 11 -> 11, of which waited for: 9 -> 5; matrix products, arithmetic and copies ran while one was open for 1% -> 0% of each run, Pallas kernels for 0% -> 18%
where the time goes in v2:
time: 60.6 us; the launch traced here: 60.4 us
  waiting for transfers between devices  25.8 us (43%)
  Pallas kernels  17.9 us (30%)
  starting transfers between devices  13.9 us (23%)
  local copies, waits for them, and re-layouts  2.61 us (4%)
    ppermute x4, waiting for transfers between devices, exchange(): got = lax.ppermute(payload, ('side', 'blk'), cycle)  24.5 us
    pallas_call x13, Pallas kernels, call(): pl.pallas_call(kernel, out_shape=shapes if many else shapes[0], in_specs=...  17.9 us
    ppermute x7, starting transfers between devices, swap(): return lax.ppermute(value, 'side', [(0, 1), (1, 0)])  13.2 us
    unnamed x8, local copies, waits for them, and re-layouts  2.58 us
    ppermute x7, waiting for transfers between devices, swap(): return lax.ppermute(value, 'side', [(0, 1), (1, 0)])  1.27 us
  transfers between devices with their start and end apart: 11, of which 5 were waited for; matrix products, arithmetic and copies ran while one was open for 0% of the time, Pallas kernels for 18%

profile of v2, /device:TPU:29, one launch (start us, length us, event | category | flops | bytes accessed | tf_op | source)
XLA Modules:
  0.0 60.4 jit_solution(4366327100367067601)
XLA Ops:
  0.0 0.7 %collective-permute-start.1 = (f32[128,768]{1,0:T(8,128)}, f32[128,768]{1,0:T(8,128)S(1)}, u32[]{:S(2)}, u32[]{:S(2)}) collective-permute-start(f32[128,768]{1,0:T(8,128)} %s_own.3), channel_id=1, source_target_pairs={{0,4},{4,0},{1,5},{5,1},{2,6},{6,2},{3,7},{7,3},{8,12},{12,8},{9,1... | collective-permute-start | bytes 1179656 | tf_op jit(solution)/shard_map/ppermute | solution.py:255
  1.3 1.3 %collective-permute-done.pattern.refs_1_.pat_oth = s32[1,6]{1,0:T(1,128)S(1)} collective-permute-done((s32[1,6]{1,0:T(1,128)}, s32[1,6]{1,0:T(1,128)S(1)}, u32[]{:S(2)}, u32[]{:S(2)}) %collective-permute-start) | collective-permute-done | bytes 56 | tf_op jit(solution)/shard_map/ppermute | solution.py:255
  2.5 1.0 %copy-done = f32[128,768]{1,0:T(8,128)S(1)} copy-done((f32[128,768]{1,0:T(8,128)S(1)}, f32[128,768]{1,0:T(8,128)}, u32[]{:S(2)}) %copy-start) | copy-done | bytes 393240
  3.5 0.9 %copy-done.2 = f32[128,384]{1,0:T(8,128)S(1)} copy-done((f32[128,384]{1,0:T(8,128)S(1)}, f32[128,384]{1,0:T(8,128)}, u32[]{:S(2)}) %copy-start.2) | copy-done | bytes 196632
  5.2 6.1 %collective-permute-done.3.s_got.z_got = f32[256,512]{1,0:T(8,128)S(1)} collective-permute-done((f32[256,512]{1,0:T(8,128)S(1)}, f32[256,512]{1,0:T(8,128)S(1)}, u32[]{:S(2)}, u32[]{:S(2)}) %collective-permute-start.3) | collective-permute-done | bytes 524320 | tf_op jit(solution)/shard_map/ppermute | solution.py:258
  11.4 3.3 %collective-permute-start.4 = (f32[256,512]{1,0:T(8,128)S(1)}, f32[256,512]{1,0:T(8,128)S(1)}, u32[]{:S(2)}, u32[]{:S(2)}) collective-permute-start(f32[256,512]{1,0:T(8,128)S(1)} %collective-permute-done.3.s_got.z_got), channel_id=1, source_target_pairs={{0,4},{4,0},{1,5},{5,1},{2,6},{6,2},{3,7},{7,3},{8,12},{12,8},{9,1... | collective-permute-start | bytes 1572872 | tf_op jit(solution)/shard_map/ppermute | solution.py:255
  14.6 1.1 %shard_map.38 = (f32[256,256]{1,0:T(8,128)S(1)}, f32[256,256]{1,0:T(8,128)S(1)}, f32[256,256]{1,0:T(8,128)S(1)}, f32[256,256]{1,0:T(8,128)S(1)}, f32[256,256]{1,...) custom-call(s32[3]{0:T(128)S(1)} %pad_add_fusion.place, ...), custom_call_target="tpu_custom_call" | custom-call | flops 1000000000 | tf_op jit(solution)/shard_map/pallas_call | solution.py:230
  15.8 1.3 %shard_map.39 = (f32[256,256]{1,0:T(8,128)S(1)}, f32[256,256]{1,0:T(8,128)S(1)}, f32[256,256]{1,0:T(8,128)S(1)}) custom-call(s32[3]{0:T(128)S(1)} %pad_add_fusion.place, f32[256,512]{1,0:T(8,128)S(1)} %collective-permute-done.3.s_got.z_got, f32[256,512]{1,0:T(8,128)S(1)} %collective-permute-done.3.s_got.z_got, f32[256,256]{1,0:T(8,128)S(1)} %get-tuple-element.41.sn, ...), custom_call_target="tpu_custom_call" | custom-call | flops 1000000000 | tf_op jit(solution)/shard_map/pallas_call | solution.py:230
  17.1 1.5 %shard_map.40 = (f32[256,256]{1,0:T(8,128)S(1)}, f32[512,256]{1,0:T(8,128)S(1)}) custom-call(s32[3]{0:T(128)S(1)} %pad_add_fusion.place, f32[256,512]{1,0:T(8,128)S(1)} %collective-permute-done.4.s_got.z_got, f32[256,512]{1,0:T(8,128)S(1)} %collective-permute-done.4.s_got.z_got, f32[256,256]{1,0:T(8,128)S(1)} %get-tuple-element.37.sf, ...), custom_call_target="tpu_custom_call" | custom-call | flops 1000000000 | tf_op jit(solution)/shard_map/pallas_call | solution.py:230
  18.7 6.1 %collective-permute-done.5.refs_2_ = f32[512,256]{1,0:T(8,128)S(1)} collective-permute-done((f32[512,256]{1,0:T(8,128)S(1)}, f32[512,256]{1,0:T(8,128)S(1)}, u32[]{:S(2)}, u32[]{:S(2)}) %collective-permute-start.5) | collective-permute-done | bytes 524320 | tf_op jit(solution)/shard_map/ppermute | solution.py:258
  24.9 2.9 %collective-permute-start.6 = (f32[512,256]{1,0:T(8,128)S(1)}, f32[512,256]{1,0:T(8,128)S(1)}, u32[]{:S(2)}, u32[]{:S(2)}) collective-permute-start(f32[512,256]{1,0:T(8,128)S(1)} %collective-permute-done.5.refs_2_), channel_id=1, source_target_pairs={{0,4},{4,0},{1,5},{5,1},{2,6},{6,2},{3,7},{7,3},{8,12},{12,8},{9,1... | collective-permute-start | bytes 1572872 | tf_op jit(solution)/shard_map/ppermute | solution.py:255
  27.8 1.8 %shard_map.41 = (f32[256,256]{1,0:T(8,128)S(1)}, f32[256,256]{1,0:T(8,128)S(1)}, f32[256,256]{1,0:T(8,128)S(1)}) custom-call(s32[3]{0:T(128)S(1)} %pad_add_fusion.place, f32[256,256]{1,0:T(8,128)S(1)} %get-tuple-element.47.zn.refs_3_, f32[256,256]{1,0:T(8,128)S(1)} %get-tuple-element.38.zm.refs_4_, f32[256,256]{1,0:T(8,128)S(1)} %get-tuple-element.39.zf, ...), custom_call_target="tpu_custom_call" | custom-call | flops 1000000000 | tf_op jit(solution)/shard_map/pallas_call | solution.py:230
  30.2 1.5 %shard_map.42 = (f32[256,256]{1,0:T(8,128)S(1)}, f32[256,256]{1,0:T(8,128)S(1)}) custom-call(s32[3]{0:T(128)S(1)} %pad_add_fusion.place, s32[1,6]{1,0:T(1,128)S(1)} %copy-done.3, s32[1,6]{1,0:T(1,128)S(1)} %collective-permute-done.pattern.refs_1_.pat_oth, f32[512,256]{1,0:T(8,128)S(1)} %collective-permute-done.5.refs_2_, ...), custom_call_target="tpu_custom_call" | custom-call | flops 1000000000 | tf_op jit(solution)/shard_map/pallas_call | solution.py:230
  31.8 1.5 %shard_map.43 = f32[256,512]{1,0:T(8,128)S(1)} custom-call(s32[3]{0:T(128)S(1)} %pad_add_fusion.place, s32[1,6]{1,0:T(1,128)S(1)} %copy-done.3, s32[1,6]{1,0:T(1,128)S(1)} %collective-permute-done.pattern.refs_1_.pat_oth, f32[512,256]{1,0:T(8,128)S(1)} %collective-permute-done.6.got, f32[256,256]{1,0:T(8,128)S(1)} %get-tuple-element.38.zm.refs_4_, ...), custom_call_target="tpu_custom_call" | custom-call | flops 1000000000 | tf_op jit(solution)/shard_map/pallas_call | solution.py:230
  33.5 6.1 %collective-permute-done.7.z_got = f32[256,512]{1,0:T(8,128)S(1)} collective-permute-done((f32[256,512]{1,0:T(8,128)S(1)}, f32[256,512]{1,0:T(8,128)S(1)}, u32[]{:S(2)}, u32[]{:S(2)}) %collective-permute-start.7) | collective-permute-done | bytes 524320 | tf_op jit(solution)/shard_map/ppermute | solution.py:258
  39.6 2.9 %collective-permute-start.8 = (f32[256,512]{1,0:T(8,128)S(1)}, f32[256,512]{1,0:T(8,128)S(1)}, u32[]{:S(2)}, u32[]{:S(2)}) collective-permute-start(f32[256,512]{1,0:T(8,128)S(1)} %collective-permute-done.7.z_got), channel_id=1, source_target_pairs={{0,4},{4,0},{1,5},{5,1},{2,6},{6,2},{3,7},{7,3},{8,12},{12,8},{9,1... | collective-permute-start | bytes 1572872 | tf_op jit(solution)/shard_map/ppermute | solution.py:255
  42.6 1.1 %shard_map.44 = (f32[256,256]{1,0:T(8,128)S(1)}, f32[256,256]{1,0:T(8,128)S(1)}, f32[256,256]{1,0:T(8,128)S(1)}) custom-call(s32[3]{0:T(128)S(1)} %pad_add_fusion.place, f32[256,256]{1,0:T(8,128)S(1)} %get-tuple-element.41.sn, f32[256,256]{1,0:T(8,128)S(1)} %get-tuple-element.54.sm, f32[256,256]{1,0:T(8,128)S(1)} %get-tuple-element.37.sf, ...), custom_call_target="tpu_custom_call" | custom-call | flops 1000000000 | tf_op jit(solution)/shard_map/pallas_call | solution.py:230
  43.6 1.3 %shard_map.45 = (f32[256,256]{1,0:T(8,128)S(1)}, f32[256,256]{1,0:T(8,128)S(1)}, f32[256,256]{1,0:T(8,128)S(1)}) custom-call(s32[3]{0:T(128)S(1)} %pad_add_fusion.place, f32[256,512]{1,0:T(8,128)S(1)} %collective-permute-done.3.s_got.z_got, f32[256,512]{1,0:T(8,128)S(1)} %collective-permute-done.7.z_got, f32[256,256]{1,0:T(8,128)S(1)} %get-tuple-element.41.sn, ...), custom_call_target="tpu_custom_call" | custom-call | flops 1000000000 | tf_op jit(solution)/shard_map/pallas_call | solution.py:230
  44.9 1.5 %shard_map.46 = (f32[256,256]{1,0:T(8,128)S(1)}, f32[512,256]{1,0:T(8,128)S(1)}) custom-call(s32[3]{0:T(128)S(1)} %pad_add_fusion.place, f32[256,512]{1,0:T(8,128)S(1)} %collective-permute-done.4.s_got.z_got, f32[256,512]{1,0:T(8,128)S(1)} %collective-permute-done.8.z_got, f32[256,256]{1,0:T(8,128)S(1)} %get-tuple-element.37.sf, ...), custom_call_target="tpu_custom_call" | custom-call | flops 1000000000 | tf_op jit(solution)/shard_map/pallas_call | solution.py:230
  46.6 6.1 %collective-permute-done.9.refs_1_ = f32[512,256]{1,0:T(8,128)S(1)} collective-permute-done((f32[512,256]{1,0:T(8,128)S(1)}, f32[512,256]{1,0:T(8,128)S(1)}, u32[]{:S(2)}, u32[]{:S(2)}) %collective-permute-start.9) | collective-permute-done | bytes 524320 | tf_op jit(solution)/shard_map/ppermute | solution.py:258
  52.7 2.9 %collective-permute-start.10 = (f32[512,256]{1,0:T(8,128)S(1)}, f32[512,256]{1,0:T(8,128)S(1)}, u32[]{:S(2)}, u32[]{:S(2)}) collective-permute-start(f32[512,256]{1,0:T(8,128)S(1)} %collective-permute-done.9.refs_1_), channel_id=1, source_target_pairs={{0,4},{4,0},{1,5},{5,1},{2,6},{6,2},{3,7},{7,3},{8,12},{12,8},{9,1... | collective-permute-start | bytes 1572872 | tf_op jit(solution)/shard_map/ppermute | solution.py:255
  55.6 1.5 %shard_map.47 = (f32[256,256]{1,0:T(8,128)S(1)}, f32[128,256]{1,0:T(8,128)S(1)}, f32[128,256]{1,0:T(8,128)S(1)}) custom-call(s32[3]{0:T(128)S(1)} %pad_add_fusion.place, f32[256,256]{1,0:T(8,128)S(1)} %get-tuple-element.61.zn.refs_2_, f32[256,256]{1,0:T(8,128)S(1)} %get-tuple-element.70.zm.refs_3_, f32[256,256]{1,0:T(8,128)S(1)} %get-tuple-element.69.zf, ...), custom_call_target="tpu_custom_call" | custom-call | flops 1000000000 | tf_op jit(solution)/shard_map/pallas_call | solution.py:230
  57.2 1.2 %shard_map.48 = (f32[128,256]{1,0:T(8,128)S(1)}, f32[128,256]{1,0:T(8,128)S(1)}) custom-call(s32[3]{0:T(128)S(1)} %pad_add_fusion.place, s32[1,6]{1,0:T(1,128)S(1)} %copy-done.3, f32[512,256]{1,0:T(8,128)S(1)} %collective-permute-done.9.refs_1_, f32[256,256]{1,0:T(8,128)S(1)} %get-tuple-element.61.zn.refs_2_, f32[256,256]{1,0:T(8,128)S(1)} %get-tuple-element.70.zm.refs_3_, ...), custom_call_target="tpu_custom_call" | custom-call | flops 1000000000 | tf_op jit(solution)/shard_map/pallas_call | solution.py:230
  58.4 2.0 %shard_map.49 = f32[128,768]{1,0:T(8,128)} custom-call(s32[3]{0:T(128)S(1)} %pad_add_fusion.place, s32[1,6]{1,0:T(1,128)S(1)} %copy-done.3, f32[512,256]{1,0:T(8,128)S(1)} %collective-permute-done.10.got, f32[256,256]{1,0:T(8,128)S(1)} %get-tuple-element.70.zm.refs_3_, f32[256,256]{1,0:T(8,128)S(1)} %get-tuple-element.69.zf, ...), custom_call_target="tpu_custom_call" | custom-call | flops 1000000000 | tf_op jit(solution)/shard_map/pallas_call | solution.py:230
  (21 shorter events, 2.6 us)
Async XLA Ops:
  0.0 2.5 %collective-permute-start.1 = (f32[128,768]{1,0:T(8,128)}, f32[128,768]{1,0:T(8,128)S(1)}, u32[]{:S(2)}, u32[]{:S(2)}) collective-permute-start(f32[128,768]{1,0:T(8,128)} %s_own.3), channel_id=1, source_target_pairs={{0,4},{4,0},{1,5},{5,1},{2,6},{6,2},{3,7},{7,3},{8,12},{12,8},{9,1... | collective-permute-start | bytes 1179656 | tf_op jit(solution)/shard_map/ppermute | solution.py:255
  0.7 1.8 %collective-permute-start.2 = (f32[128,384]{1,0:T(8,128)}, f32[128,384]{1,0:T(8,128)S(1)}, u32[]{:S(2)}, u32[]{:S(2)}) collective-permute-start(f32[128,384]{1,0:T(8,128)} %h_own.3), channel_id=1, source_target_pairs={{0,4},{4,0},{1,5},{5,1},{2,6},{6,2},{3,7},{7,3},{8,12},{12,8},{9,1... | collective-permute-start | bytes 589832 | tf_op jit(solution)/shard_map/ppermute | solution.py:255
  0.7 1.8 %collective-permute-start = (s32[1,6]{1,0:T(1,128)}, s32[1,6]{1,0:T(1,128)S(1)}, u32[]{:S(2)}, u32[]{:S(2)}) collective-permute-start(s32[1,6]{1,0:T(1,128)} %pat_own.3), channel_id=1, source_target_pairs={{0,4},{4,0},{1,5},{5,1},{2,6},{6,2},{3,7},{7,3},{8,12},{12,8},{9,1... | collective-permute-start | bytes 80 | tf_op jit(solution)/shard_map/ppermute | solution.py:255
  2.5 1.0 %copy-start = (f32[128,768]{1,0:T(8,128)S(1)}, f32[128,768]{1,0:T(8,128)}, u32[]{:S(2)}) copy-start(f32[128,768]{1,0:T(8,128)} %s_own.3) | copy-start | bytes 1179652
  3.5 0.9 %copy-start.2 = (f32[128,384]{1,0:T(8,128)S(1)}, f32[128,384]{1,0:T(8,128)}, u32[]{:S(2)}) copy-start(f32[128,384]{1,0:T(8,128)} %h_own.3) | copy-start | bytes 589828
  4.5 10.2 %copy-start.1 = (f32[128,768]{1,0:T(8,128)S(1)}, f32[128,768]{1,0:T(8,128)}, u32[]{:S(2)}) copy-start(f32[128,768]{1,0:T(8,128)} %s_own.3) | copy-start | bytes 1179652
  5.1 6.3 %collective-permute-start.3 = (f32[256,512]{1,0:T(8,128)S(1)}, f32[256,512]{1,0:T(8,128)S(1)}, u32[]{:S(2)}, u32[]{:S(2)}) collective-permute-start(f32[256,512]{1,0:T(8,128)S(1)} %shard_map.37), channel_id=1, source_target_pairs={{0,1},{1,2},{2,3},{3,7},{5,4},{6,5},{7,6},{4,0},{8,9},{9,10},{10,1... | collective-permute-start | bytes 1572872 | tf_op jit(solution)/shard_map/ppermute | solution.py:258
  11.4 5.7 %collective-permute-start.4 = (f32[256,512]{1,0:T(8,128)S(1)}, f32[256,512]{1,0:T(8,128)S(1)}, u32[]{:S(2)}, u32[]{:S(2)}) collective-permute-start(f32[256,512]{1,0:T(8,128)S(1)} %collective-permute-done.3.s_got.z_got), channel_id=1, source_target_pairs={{0,4},{4,0},{1,5},{5,1},{2,6},{6,2},{3,7},{7,3},{8,12},{12,8},{9,1... | collective-permute-start | bytes 1572872 | tf_op jit(solution)/shard_map/ppermute | solution.py:255
  18.5 6.3 %collective-permute-start.5 = (f32[512,256]{1,0:T(8,128)S(1)}, f32[512,256]{1,0:T(8,128)S(1)}, u32[]{:S(2)}, u32[]{:S(2)}) collective-permute-start(f32[512,256]{1,0:T(8,128)S(1)} %get-tuple-element.46.pay), channel_id=1, source_target_pairs={{0,1},{1,2},{2,3},{3,7},{5,4},{6,5},{7,6},{4,0},{8,9},{9,10},{10,1... | collective-permute-start | bytes 1572872 | tf_op jit(solution)/shard_map/ppermute | solution.py:258
  24.9 6.9 %collective-permute-start.6 = (f32[512,256]{1,0:T(8,128)S(1)}, f32[512,256]{1,0:T(8,128)S(1)}, u32[]{:S(2)}, u32[]{:S(2)}) collective-permute-start(f32[512,256]{1,0:T(8,128)S(1)} %collective-permute-done.5.refs_2_), channel_id=1, source_target_pairs={{0,4},{4,0},{1,5},{5,1},{2,6},{6,2},{3,7},{7,3},{8,12},{12,8},{9,1... | collective-permute-start | bytes 1572872 | tf_op jit(solution)/shard_map/ppermute | solution.py:255
  29.6 0.7 %copy-start.3 = (s32[1,6]{1,0:T(1,128)S(1)}, s32[1,6]{1,0:T(1,128)}, u32[]{:S(2)}) copy-start(s32[1,6]{1,0:T(1,128)} %pat_own.3) | copy-start | bytes 76
  33.3 6.3 %collective-permute-start.7 = (f32[256,512]{1,0:T(8,128)S(1)}, f32[256,512]{1,0:T(8,128)S(1)}, u32[]{:S(2)}, u32[]{:S(2)}) collective-permute-start(f32[256,512]{1,0:T(8,128)S(1)} %shard_map.43), channel_id=1, source_target_pairs={{0,1},{1,2},{2,3},{3,7},{5,4},{6,5},{7,6},{4,0},{8,9},{9,10},{10,1... | collective-permute-start | bytes 1572872 | tf_op jit(solution)/shard_map/ppermute | solution.py:258
  39.6 5.3 %collective-permute-start.8 = (f32[256,512]{1,0:T(8,128)S(1)}, f32[256,512]{1,0:T(8,128)S(1)}, u32[]{:S(2)}, u32[]{:S(2)}) collective-permute-start(f32[256,512]{1,0:T(8,128)S(1)} %collective-permute-done.7.z_got), channel_id=1, source_target_pairs={{0,4},{4,0},{1,5},{5,1},{2,6},{6,2},{3,7},{7,3},{8,12},{12,8},{9,1... | collective-permute-start | bytes 1572872 | tf_op jit(solution)/shard_map/ppermute | solution.py:255
  46.4 6.3 %collective-permute-start.9 = (f32[512,256]{1,0:T(8,128)S(1)}, f32[512,256]{1,0:T(8,128)S(1)}, u32[]{:S(2)}, u32[]{:S(2)}) collective-permute-start(f32[512,256]{1,0:T(8,128)S(1)} %get-tuple-element.60.pay), channel_id=1, source_target_pairs={{0,1},{1,2},{2,3},{3,7},{5,4},{6,5},{7,6},{4,0},{8,9},{9,10},{10,1... | collective-permute-start | bytes 1572872 | tf_op jit(solution)/shard_map/ppermute | solution.py:258
  52.7 5.7 %collective-permute-start.10 = (f32[512,256]{1,0:T(8,128)S(1)}, f32[512,256]{1,0:T(8,128)S(1)}, u32[]{:S(2)}, u32[]{:S(2)}) collective-permute-start(f32[512,256]{1,0:T(8,128)S(1)} %collective-permute-done.9.refs_1_), channel_id=1, source_target_pairs={{0,4},{4,0},{1,5},{5,1},{2,6},{6,2},{3,7},{7,3},{8,12},{12,8},{9,1... | collective-permute-start | bytes 1572872 | tf_op jit(solution)/shard_map/ppermute | solution.py:255

commit v3 on v2

v3 whole, which is shorter than its diff:
```python
import jax
import jax.numpy as jnp
from jax import lax
from jax.experimental import pallas as pl
from jax.experimental.pallas import tpu as pltpu
from jax.sharding import PartitionSpec as P


ITERS = 2
BF = jnp.bfloat16
F32 = jnp.float32


def halves_of(value):
    high = value.astype(BF)
    low = (value - high.astype(F32)).astype(BF)
    return high, low


def product(left, right, dims):
    (lh, ll), (rh, rl) = left, right

    def dot(a, b):
        return lax.dot_general(a, b, (dims, ((), ())), preferred_element_type=F32)

    return dot(lh, rh) + (dot(lh, rl) + dot(ll, rh))


def nn(left, right):
    return product(left, right, ((1,), (0,)))


def tn(left, right):
    return product(left, right, ((0,), (0,)))


def ordered(side, own, other):
    return jnp.where(side == 0, own, other), jnp.where(side == 0, other, own)


def block_diag(top, bottom):
    zero = jnp.zeros_like(top)
    return jnp.concatenate(
        [jnp.concatenate([top, zero], axis=1), jnp.concatenate([zero, bottom], axis=1)], axis=0
    )


def oriented(side, row, width):
    first, middle, final = [row[:, e * width:(e + 1) * width] for e in range(3)]
    near, far = ordered(side, first, final)
    return near, middle, far


def pack(value):
    rows = value.shape[0] // 2
    return jnp.concatenate([value[:rows, :rows], value[:rows, rows:], value[rows:, rows:]], axis=1)


def unpack(cells):
    rows = cells.shape[0]
    first, cross, final = [cells[:, e * rows:(e + 1) * rows] for e in range(3)]
    return jnp.concatenate(
        [jnp.concatenate([first, cross], axis=1), jnp.concatenate([cross.T, final], axis=1)], axis=0
    )


def stage_kernel(place, pat_own, s_own, h_own, s_out, h_out):
    width = s_out.shape[1]
    s_out[...] = s_own[:, width:2 * width]
    h_out[...] = h_own[...]


def start_kernel(place, pattern, s_own, s_oth, h_own, h_oth, pay_a, pay_b):
    side = place[0]
    rows = s_own.shape[0]
    width = 2 * rows
    top, bottom = ordered(side, s_own[...], s_oth[:, width:2 * width])
    pay_a[:, :width] = top
    pay_a[:, width:3 * rows] = bottom[:, rows:]
    top, bottom = ordered(side, h_own[...], h_oth[...])
    for e, part in enumerate((top, bottom)):
        _, middle, far = oriented(side, part, rows)
        pay_a[:, (3 + e) * rows:(4 + e) * rows] = far
        pay_b[:, e * rows:(e + 1) * rows] = middle


def image_local(s_row, z_mid, outs):
    near, middle, far = [halves_of(v) for v in s_row]
    z = halves_of(z_mid)
    outs[0][...] = tn(near, z)
    outs[1][...] = nn(middle, z)
    outs[2][...] = tn(far, z)


def first_local_kernel(place, s_own, s_oth, h_own, h_oth, sn, sm, sf, zn, zm, zf, tn_, tm, tf):
    side = place[0]
    rows = s_own.shape[0]
    width = 2 * rows
    s_all = jnp.concatenate(ordered(side, s_own[...], s_oth[...]), axis=0)
    s_row = oriented(side, s_all, width)
    top, bottom = ordered(side, h_own[...], h_oth[...])
    z_row = [block_diag(a, b) for a, b in zip(oriented(side, top, rows), oriented(side, bottom, rows))]
    for ref, v in zip((sn, sm, sf, zn, zm, zf), [*s_row, *z_row]):
        ref[...] = v
    image_local(s_row, z_row[1], (tn_, tm, tf))


def next_local_kernel(place, sn, sm, sf, zm, tn_, tm, tf):
    image_local((sn[...], sm[...], sf[...]), zm[...], (tn_, tm, tf))


def masked(ref, keep):
    return jnp.where(keep == 1, ref[...], 0.0)


def off_part(ref, keep, wide):
    got = masked(ref, keep)
    if wide:
        return halves_of(got)
    rows = got.shape[0]
    return halves_of(block_diag(got[:, 3 * rows:4 * rows], got[:, 4 * rows:]))


def diag_part(ref, keep, wide):
    got = masked(ref, keep)
    if wide:
        return halves_of(got)
    rows = got.shape[0]
    return halves_of(block_diag(got[:, :rows], got[:, rows:]))


def overlap_part(ref, keep):
    got = masked(ref, keep)
    return halves_of(unpack(got[:, :3 * got.shape[0]]))


def near_image_kernel(wide):
    def kernel(place, s_got, z_got, sn, t_near, t_mid, mid_ref, image_ref, e_mid):
        off = off_part(z_got, place[1], wide)
        image = nn(overlap_part(s_got, place[1]), off) + t_near[...]
        image_ref[...] = image
        mid_ref[...] = t_mid[...] + nn(halves_of(sn[...]), off)
        e_mid[...] = tn(off, halves_of(image))

    return kernel


def far_image_kernel(wide):
    def kernel(place, s_got, z_got, sf, zm, zf, t_far, mid_part, e_mid, mid_ref, image_ref, e_far, d_ref, pay_ref):
        width = t_far.shape[0]
        off = off_part(z_got, place[2], wide)
        middle = mid_part[...] + nn(halves_of(sf[...]), off)
        mid_ref[...] = middle
        middle = halves_of(middle)
        image = nn(overlap_part(s_got, place[2]), off) + t_far[...]
        image_ref[...] = image
        row_ids = lax.broadcasted_iota(jnp.int32, (width, width), 0)
        col_ids = lax.broadcasted_iota(jnp.int32, (width, width), 1)
        eye = (row_ids == col_ids).astype(F32)
        delta = eye - (e_mid[...] + tn(halves_of(zm[...]), middle) + tn(off, halves_of(image)))
        d_ref[...] = delta
        pay_ref[...] = pack(delta)
        e_far[...] = tn(halves_of(zf[...]), middle)

    return kernel


def near_delta_kernel(wide):
    def kernel(place, z_got, image, zn, mid, d_near):
        diag = diag_part(z_got, place[1], wide)
        d_near[...] = -(tn(halves_of(zn[...]), halves_of(mid[...])) + tn(diag, halves_of(image[...])))

    return kernel


def far_delta_kernel(wide):
    def kernel(place, z_got, image, e_far, d_far):
        diag = diag_part(z_got, place[2], wide)
        d_far[...] = -(e_far[...] + tn(diag, halves_of(image[...])))

    return kernel


def own_rows(ref, side, rows):
    if ref.shape[0] == rows:
        return ref[...]
    return jnp.where(side == 0, ref[:rows, :], ref[rows:, :])


def mid_first_kernel(place, zn, zm, zf, d_near, d_mid, d_far, first_ref, part_ref):
    side = place[0]
    rows = first_ref.shape[0]
    middle = halves_of(d_mid[...])
    first = nn(halves_of(own_rows(zn, side, rows)), halves_of(d_near[...]))
    first += nn(halves_of(own_rows(zm, side, rows)), middle)
    first += nn(halves_of(own_rows(zf, side, rows)), halves_of(d_far[...]))
    first_ref[...] = first
    part_ref[...] = nn(halves_of(first), middle)


def diag_kernel(place, d_own, d_oth, zn, zf, near_ref, far_ref, diag_near, diag_far):
    side = place[0]
    rows = near_ref.shape[0]
    for keep, got, z, ref, full in ((place[1], d_own, zn, near_ref, diag_near), (place[2], d_oth, zf, far_ref, diag_far)):
        diag = unpack(masked(got, keep))
        full[...] = diag
        ref[...] = nn(halves_of(own_rows(z, side, rows)), halves_of(diag))


def kept(values, pats, side, slot, rows):
    count = pats[0].shape[0]
    tile = rows // count
    both = values.shape[0] != rows
    bands = []
    for f in range(2 if both else 1):
        half = f if both else side
        for i in range(count):
            cells = []
            for q in range(2 * count):
                at = slot * 2 * count + q
                bit = jnp.where(side == f, pats[0][i, at], pats[1][i, at]) if both else pats[0][i, at]
                flag = jnp.logical_or(bit == 1, (2 + half) * count + i == at)
                top = (f * count + i) * tile
                cell = values[top:top + tile, q * tile:(q + 1) * tile]
                cells.append(jnp.where(flag, 1.0, 0.0) * cell)
            bands.append(jnp.concatenate(cells, axis=1))
    return jnp.concatenate(bands, axis=0) if len(bands) > 1 else bands[0]


def side_products(got, keep, diag, z_diag, z_mid, first):
    off = halves_of(masked(got, keep))
    outer = z_diag[...] + nn(halves_of(z_mid), off)
    split = halves_of(outer)
    second = nn(split, halves_of(diag[...])) + nn(halves_of(first[...]), off)
    return outer, split, second


def near_factor_kernel(place, *refs):
    pats, (got, diag, z_diag, zn, zm, first, part, d_near, new_ref, part_ref) = refs[:-10], refs[-10:]
    side = place[0]
    rows = zn.shape[0] // 2
    size = first.shape[0]
    outer, split, second = side_products(got, place[1], diag, z_diag, own_rows(zm, side, size), first)
    part_ref[...] = part[...] + nn(split, halves_of(d_near[...]))
    z = own_rows(zn, side, size)
    new_ref[...] = kept(z + 0.5 * outer + 0.375 * second, pats, side, 2 * side, rows)


def far_blocks(place, pats, got, diag, z_diag, zm, zf, first, part, d_far):
    side = place[0]
    rows = zm.shape[0] // 2
    size = first.shape[0]
    z, mid = own_rows(zf, side, size), own_rows(zm, side, size)
    outer, split, second = side_products(got, place[2], diag, z_diag, mid, first)
    second_mid = part[...] + nn(split, halves_of(d_far[...]))
    far = kept(z + 0.5 * outer + 0.375 * second, pats, side, 2 - 2 * side, rows)
    return kept(mid + 0.5 * first[...] + 0.375 * second_mid, pats, side, 1, rows), far


def far_factor_kernel(place, pat_own, pat_oth, *refs):
    refs[-2][...], refs[-1][...] = far_blocks(place, (pat_own, pat_oth), *refs[:-2])


def last_factor_kernel(place, pat_own, *refs):
    near, out_ref = refs[-2:]
    width = near.shape[1]
    middle, far = far_blocks(place, (pat_own,), *refs[:-2])
    low, high = ordered(place[0], near[...], far)
    out_ref[:, :width] = low
    out_ref[:, width:2 * width] = middle
    out_ref[:, 2 * width:] = high


def call(kernel, outs, scalars, arrays, flops=10**9):
    smem = pl.BlockSpec(memory_space=pltpu.SMEM)
    vmem = pl.BlockSpec(memory_space=pltpu.VMEM)
    shapes = [jax.ShapeDtypeStruct(s, F32) for s in outs]
    many = len(shapes) > 1
    return pl.pallas_call(
        kernel,
        out_shape=shapes if many else shapes[0],
        in_specs=[smem] * len(scalars) + [vmem] * len(arrays),
        out_specs=[vmem] * len(shapes) if many else vmem,
        cost_estimate=pl.CostEstimate(flops=flops, bytes_accessed=0, transcendentals=0),
        compiler_params=pltpu.CompilerParams(vmem_limit_bytes=16 * 2**20),
    )(*scalars, *arrays)


def per_device(intersect, half_factors, z_pattern):
    rows = intersect.shape[0]
    width = 2 * rows
    square = (width, width)
    count = lax.axis_size("blk")
    last = count - 1
    side = lax.axis_index("side")
    blk = lax.axis_index("blk")
    inner = jnp.stack([blk > 0, blk < last])
    place = jnp.stack([side, jnp.where(side == 0, inner[0], inner[1]), jnp.where(side == 0, inner[1], inner[0])])
    place = place.astype(jnp.int32)
    cycle = [(i, i + 1) for i in range(last)] + [(last, count + last)]
    cycle += [(count + i + 1, count + i) for i in range(last)] + [(count, 0)]

    def swap(value):
        return lax.ppermute(value, "side", [(0, 1), (1, 0)])

    def exchange(payload):
        got = lax.ppermute(payload, ("side", "blk"), cycle)
        return got, swap(got)

    s_oth, h_oth, p_oth = swap(intersect), swap(half_factors), swap(z_pattern)
    s_mid, h_own = call(stage_kernel, [(rows, width), (rows, 3 * rows)], [place, z_pattern], [intersect, half_factors])
    off, diag = call(start_kernel, [(rows, 5 * rows), (rows, width)], [place, p_oth], [s_mid, s_oth, h_own, h_oth])
    s_near, s_far = z_near, z_far = exchange(off)
    g_near, g_far = exchange(diag)
    sn, sm, sf, zn, zm, zf, t_near, t_mid, t_far = call(
        first_local_kernel, [square] * 9, [place], [intersect, s_oth, h_own, h_oth])
    for step in range(ITERS):
        final, wide = step == ITERS - 1, step > 0
        if wide:
            z_near, z_far = exchange(zf)
            g_near, g_far = exchange(zm)
            t_near, t_mid, t_far = call(next_local_kernel, [square] * 3, [place], [sn, sm, sf, zm])
        mid, i_near, e_mid = call(
            near_image_kernel(wide), [square] * 3, [place], [s_near, z_near, sn, t_near, t_mid])
        mid, i_far, e_far, d_mid, diag = call(
            far_image_kernel(wide), [square] * 4 + [(rows, 3 * rows)], [place],
            [s_far, z_far, sf, zm, zf, t_far, mid, e_mid])
        g_own, g_oth = exchange(diag)
        d_near = call(near_delta_kernel(wide), [square], [place], [g_near, i_near, zn, mid])
        d_far = call(far_delta_kernel(wide), [square], [place], [g_far, i_far, e_far])
        d_own, d_oth = exchange(d_far)
        band = (rows if final else width, width)
        pats = [z_pattern] if final else [z_pattern, p_oth]
        first, part = call(
            mid_first_kernel, [band, band], [place], [zn, zm, zf, d_near, d_mid, d_far])
        z_dn, z_df, diag_n, diag_f = call(
            diag_kernel, [band, band, square, square], [place], [g_own, g_oth, zn, zf])
        near, part = call(
            near_factor_kernel, [band, band], [place] + pats,
            [d_own, diag_n, z_dn, zn, zm, first, part, d_near])
        rest = [d_oth, diag_f, z_df, zm, zf, first, part, d_far]
        if final:
            return call(last_factor_kernel, [(rows, 3 * width)], [place] + pats, rest + [near])
        zm, zf = call(far_factor_kernel, [square, square], [place] + pats, rest)
        zn = near


def solution(mesh):
    spec = P(("pair", "side", "blk"), None)
    return jax.shard_map(
        per_device,
        mesh=mesh,
        in_specs=(spec, spec, spec),
        out_specs=spec,
        check_vma=False,
    )
```

time: 60.6 us -> 60.7 us (level); the launches traced: 60.4 us -> 59.8 us
  waiting for transfers between devices: 25.8 us -> 11.4 us
  starting transfers between devices: 13.9 us -> 23.2 us
  Pallas kernels: 17.9 us -> 22.4 us
    ppermute x4 -> x8, waiting for transfers between devices: 24.5 us -> 11.3 us  [exchange(): got = lax.ppermute(payload, ('side', 'blk'), cycle)]
    ppermute x7 -> x11, starting transfers between devices: 13.2 us -> 21 us  [swap(): return lax.ppermute(value, 'side', [(0, 1), (1, 0)])]
    pallas_call x13 -> x20, Pallas kernels: 17.9 us -> 22.4 us  [call(): pl.pallas_call(kernel, out_shape=shapes if many else shapes[0], in_specs=...]
    ppermute x4 -> x8, starting transfers between devices: 0.71 us -> 2.17 us  [exchange(): got = lax.ppermute(payload, ('side', 'blk'), cycle)]
    ppermute x7 -> x11, waiting for transfers between devices: 1.27 us -> 0.03 us  [swap(): return lax.ppermute(value, 'side', [(0, 1), (1, 0)])]
  transfers between devices with their start and end apart: 11 -> 19, of which waited for: 5 -> 6; matrix products, arithmetic and copies ran while one was open for 0% -> 0% of each run, Pallas kernels for 18% -> 31%
where the time goes in v3:
time: 60.7 us; the launch traced here: 59.8 us
  starting transfers between devices  23.2 us (38%)
  Pallas kernels  22.4 us (37%)
  waiting for transfers between devices  11.4 us (19%)
  local copies, waits for them, and re-layouts  2.51 us (4%)
    pallas_call x20, Pallas kernels, call(): pl.pallas_call(kernel, out_shape=shapes if many else shapes[0], in_specs=...  22.4 us
    ppermute x11, starting transfers between devices, swap(): return lax.ppermute(value, 'side', [(0, 1), (1, 0)])  21 us
    ppermute x8, waiting for transfers between devices, exchange(): got = lax.ppermute(payload, ('side', 'blk'), cycle)  11.3 us
    unnamed x8, local copies, waits for them, and re-layouts  2.51 us
    ppermute x8, starting transfers between devices, exchange(): got = lax.ppermute(payload, ('side', 'blk'), cycle)  2.17 us
  transfers between devices with their start and end apart: 19, of which 6 were waited for; matrix products, arithmetic and copies ran while one was open for 0% of the time, Pallas kernels for 31%

profile of v3, /device:TPU:29, one launch (start us, length us, event | category | flops | bytes accessed | tf_op | source)
XLA Modules:
  0.0 59.8 jit_solution(11751591092649195377)
XLA Ops:
  5.2 4.0 %collective-permute-done.5.s_got.z_got = f32[128,640]{1,0:T(8,128)S(1)} collective-permute-done((f32[128,640]{1,0:T(8,128)S(1)}, f32[128,640]{1,0:T(8,128)S(1)}, u32[]{:S(2)}, u32[]{:S(2)}) %collective-permute-start.5) | collective-permute-done | bytes 327712 | tf_op jit(solution)/shard_map/ppermute | solution.py:307
  9.2 2.9 %collective-permute-start.6 = (f32[128,640]{1,0:T(8,128)S(1)}, f32[128,640]{1,0:T(8,128)S(1)}, u32[]{:S(2)}, u32[]{:S(2)}) collective-permute-start(f32[128,640]{1,0:T(8,128)S(1)} %collective-permute-done.5.s_got.z_got), channel_id=1, source_target_pairs={{0,4},{4,0},{1,5},{5,1},{2,6},{6,2},{3,7},{7,3},{8,12},{12,8},{9,1... | collective-permute-start | bytes 983048 | tf_op jit(solution)/shard_map/ppermute | solution.py:304
  12.3 1.1 %shard_map.39 = (f32[256,256]{1,0:T(8,128)S(1)}, f32[256,256]{1,0:T(8,128)S(1)}, f32[256,256]{1,0:T(8,128)S(1)}, f32[256,256]{1,0:T(8,128)S(1)}, f32[256,256]{1,...) custom-call(s32[3]{0:T(128)S(1)} %pad_add_fusion.place, ...), custom_call_target="tpu_custom_call" | custom-call | flops 1000000000 | tf_op jit(solution)/shard_map/pallas_call | solution.py:279
  14.2 2.9 %collective-permute-start.4 = (f32[128,256]{1,0:T(8,128)S(1)}, f32[128,256]{1,0:T(8,128)S(1)}, u32[]{:S(2)}, u32[]{:S(2)}) collective-permute-start(f32[128,256]{1,0:T(8,128)S(1)} %collective-permute-done.3.z_got), channel_id=1, source_target_pairs={{0,4},{4,0},{1,5},{5,1},{2,6},{6,2},{3,7},{7,3},{8,12},{12,8},{9,1... | collective-permute-start | bytes 393224 | tf_op jit(solution)/shard_map/ppermute | solution.py:304
  17.1 1.2 %shard_map.40 = (f32[256,256]{1,0:T(8,128)S(1)}, f32[256,256]{1,0:T(8,128)S(1)}, f32[256,256]{1,0:T(8,128)S(1)}) custom-call(s32[3]{0:T(128)S(1)} %pad_add_fusion.place, f32[128,640]{1,0:T(8,128)S(1)} %collective-permute-done.5.s_got.z_got, f32[128,640]{1,0:T(8,128)S(1)} %collective-permute-done.5.s_got.z_got, f32[256,256]{1,0:T(8,128)S(1)} %get-tuple-element.63.sn, ...), custom_call_target="tpu_custom_call" | custom-call | flops 1000000000 | tf_op jit(solution)/shard_map/pallas_call | solution.py:279
  18.2 1.4 %shard_map.41 = (f32[256,256]{1,0:T(8,128)S(1)}, f32[256,256]{1,0:T(8,128)S(1)}, f32[256,256]{1,0:T(8,128)S(1)}, f32[256,256]{1,0:T(8,128)S(1)}, f32[128,384]{1,0:T(8,128)S(1)}) custom-call(s32[3]{0:T(128)S(1)} %pad_add_fusion.place, f32[128,640]{1,0:T(8,128)S(1)} %collective-permute-done.6.s_got.z_got, f32[128,640]{1,0:T(8,128)S(1)} %collective-permute-done.6.s_got.z_got, ...), custom_call_target="tpu_custom_call" | custom-call | flops 1000000000 | tf_op jit(solution)/shard_map/pallas_call | solution.py:279
  20.8 1.6 %collective-permute-done.9.d_own = f32[128,384]{1,0:T(8,128)S(1)} collective-permute-done((f32[128,384]{1,0:T(8,128)S(1)}, f32[128,384]{1,0:T(8,128)S(1)}, u32[]{:S(2)}, u32[]{:S(2)}) %collective-permute-start.9) | collective-permute-done | bytes 196640 | tf_op jit(solution)/shard_map/ppermute | solution.py:307
  22.4 2.9 %collective-permute-start.10 = (f32[128,384]{1,0:T(8,128)S(1)}, f32[128,384]{1,0:T(8,128)S(1)}, u32[]{:S(2)}, u32[]{:S(2)}) collective-permute-start(f32[128,384]{1,0:T(8,128)S(1)} %collective-permute-done.9.d_own), channel_id=1, source_target_pairs={{0,4},{4,0},{1,5},{5,1},{2,6},{6,2},{3,7},{7,3},{8,12},{12,8},{9,1... | collective-permute-start | bytes 589832 | tf_op jit(solution)/shard_map/ppermute | solution.py:304
  26.3 1.8 %collective-permute-start.8 = (f32[256,256]{1,0:T(8,128)S(1)}, f32[256,256]{1,0:T(8,128)S(1)}, u32[]{:S(2)}, u32[]{:S(2)}) collective-permute-start(f32[256,256]{1,0:T(8,128)S(1)} %collective-permute-done.7.refs_2_), channel_id=1, source_target_pairs={{0,4},{4,0},{1,5},{5,1},{2,6},{6,2},{3,7},{7,3},{8,12},{12,8},{9,1... | collective-permute-start | bytes 786440 | tf_op jit(solution)/shard_map/ppermute | solution.py:304
  28.1 1.4 %shard_map.45 = (f32[256,256]{1,0:T(8,128)S(1)}, f32[256,256]{1,0:T(8,128)S(1)}) custom-call(s32[3]{0:T(128)S(1)} %pad_add_fusion.place, f32[256,256]{1,0:T(8,128)S(1)} %get-tuple-element.71.zn.refs_5_, f32[256,256]{1,0:T(8,128)S(1)} %get-tuple-element.60.zm.refs_6_.refs_3_, f32[256,256]{1,0:T(8,128)S(1)} %get-tuple-element.61.zf.refs_4_, ...), custom_call_target="tpu_custom_call" | custom-call | flops 1000000000 | tf_op jit(solution)/shard_map/pallas_call | solution.py:279
  30.5 1.4 %shard_map.46 = (f32[256,256]{1,0:T(8,128)S(1)}, f32[256,256]{1,0:T(8,128)S(1)}) custom-call(s32[3]{0:T(128)S(1)} %pad_add_fusion.place, s32[1,6]{1,0:T(1,128)S(1)} %copy-done.3, s32[1,6]{1,0:T(1,128)S(1)} %collective-permute-done.pattern.refs_1_.pat_oth, f32[256,256]{1,0:T(8,128)S(1)} %collective-permute-done.7.refs_2_, ...), custom_call_target="tpu_custom_call" | custom-call | flops 1000000000 | tf_op jit(solution)/shard_map/pallas_call | solution.py:279
  31.9 1.4 %shard_map.47 = (f32[256,256]{1,0:T(8,128)S(1)}, f32[256,256]{1,0:T(8,128)S(1)}) custom-call(s32[3]{0:T(128)S(1)} %pad_add_fusion.place, s32[1,6]{1,0:T(1,128)S(1)} %copy-done.3, s32[1,6]{1,0:T(1,128)S(1)} %collective-permute-done.pattern.refs_1_.pat_oth, f32[256,256]{1,0:T(8,128)S(1)} %collective-permute-done.8.refs_0_, ...), custom_call_target="tpu_custom_call" | custom-call | flops 1000000000 | tf_op jit(solution)/shard_map/pallas_call | solution.py:279
  34.1 3.1 %collective-permute-done.13.z_got = f32[256,256]{1,0:T(8,128)S(1)} collective-permute-done((f32[256,256]{1,0:T(8,128)S(1)}, f32[256,256]{1,0:T(8,128)S(1)}, u32[]{:S(2)}, u32[]{:S(2)}) %collective-permute-start.13) | collective-permute-done | bytes 262176 | tf_op jit(solution)/shard_map/ppermute | solution.py:307
  37.2 2.5 %collective-permute-start.14 = (f32[256,256]{1,0:T(8,128)S(1)}, f32[256,256]{1,0:T(8,128)S(1)}, u32[]{:S(2)}, u32[]{:S(2)}) collective-permute-start(f32[256,256]{1,0:T(8,128)S(1)} %collective-permute-done.13.z_got), channel_id=1, source_target_pairs={{0,4},{4,0},{1,5},{5,1},{2,6},{6,2},{3,7},{7,3},{8,12},{12,8},{9,1... | collective-permute-start | bytes 786440 | tf_op jit(solution)/shard_map/ppermute | solution.py:304
  40.0 2.5 %collective-permute-start.12 = (f32[256,256]{1,0:T(8,128)S(1)}, f32[256,256]{1,0:T(8,128)S(1)}, u32[]{:S(2)}, u32[]{:S(2)}) collective-permute-start(f32[256,256]{1,0:T(8,128)S(1)} %collective-permute-done.11.z_got), channel_id=1, source_target_pairs={{0,4},{4,0},{1,5},{5,1},{2,6},{6,2},{3,7},{7,3},{8,12},{12,8},{9,1... | collective-permute-start | bytes 786440 | tf_op jit(solution)/shard_map/ppermute | solution.py:304
  42.6 1.1 %shard_map.48 = (f32[256,256]{1,0:T(8,128)S(1)}, f32[256,256]{1,0:T(8,128)S(1)}, f32[256,256]{1,0:T(8,128)S(1)}) custom-call(s32[3]{0:T(128)S(1)} %pad_add_fusion.place, f32[256,256]{1,0:T(8,128)S(1)} %get-tuple-element.63.sn, f32[256,256]{1,0:T(8,128)S(1)} %get-tuple-element.84.sm, f32[256,256]{1,0:T(8,128)S(1)} %get-tuple-element.59.sf, ...), custom_call_target="tpu_custom_call" | custom-call | flops 1000000000 | tf_op jit(solution)/shard_map/pallas_call | solution.py:279
  43.6 1.2 %shard_map.49 = (f32[256,256]{1,0:T(8,128)S(1)}, f32[256,256]{1,0:T(8,128)S(1)}, f32[256,256]{1,0:T(8,128)S(1)}) custom-call(s32[3]{0:T(128)S(1)} %pad_add_fusion.place, f32[128,640]{1,0:T(8,128)S(1)} %collective-permute-done.5.s_got.z_got, f32[256,256]{1,0:T(8,128)S(1)} %collective-permute-done.13.z_got, f32[256,256]{1,0:T(8,128)S(1)} %get-tuple-element.63.sn, ...), custom_call_target="tpu_custom_call" | custom-call | flops 1000000000 | tf_op jit(solution)/shard_map/pallas_call | solution.py:279
  44.8 1.4 %shard_map.50 = (f32[256,256]{1,0:T(8,128)S(1)}, f32[256,256]{1,0:T(8,128)S(1)}, f32[256,256]{1,0:T(8,128)S(1)}, f32[256,256]{1,0:T(8,128)S(1)}, f32[128,384]{1,0:T(8,128)S(1)}) custom-call(s32[3]{0:T(128)S(1)} %pad_add_fusion.place, f32[128,640]{1,0:T(8,128)S(1)} %collective-permute-done.6.s_got.z_got, f32[256,256]{1,0:T(8,128)S(1)} %collective-permute-done.14.z_got, ...), custom_call_target="tpu_custom_call" | custom-call | flops 1000000000 | tf_op jit(solution)/shard_map/pallas_call | solution.py:279
  47.8 1.6 %collective-permute-done.17.d_own = f32[128,384]{1,0:T(8,128)S(1)} collective-permute-done((f32[128,384]{1,0:T(8,128)S(1)}, f32[128,384]{1,0:T(8,128)S(1)}, u32[]{:S(2)}, u32[]{:S(2)}) %collective-permute-start.17) | collective-permute-done | bytes 196640 | tf_op jit(solution)/shard_map/ppermute | solution.py:307
  49.4 2.5 %collective-permute-start.18 = (f32[128,384]{1,0:T(8,128)S(1)}, f32[128,384]{1,0:T(8,128)S(1)}, u32[]{:S(2)}, u32[]{:S(2)}) collective-permute-start(f32[128,384]{1,0:T(8,128)S(1)} %collective-permute-done.17.d_own), channel_id=1, source_target_pairs={{0,4},{4,0},{1,5},{5,1},{2,6},{6,2},{3,7},{7,3},{8,12},{12,8},{9,1... | collective-permute-start | bytes 589832 | tf_op jit(solution)/shard_map/ppermute | solution.py:304
  52.9 1.8 %collective-permute-start.16 = (f32[256,256]{1,0:T(8,128)S(1)}, f32[256,256]{1,0:T(8,128)S(1)}, u32[]{:S(2)}, u32[]{:S(2)}) collective-permute-start(f32[256,256]{1,0:T(8,128)S(1)} %collective-permute-done.15.refs_1_), channel_id=1, source_target_pairs={{0,4},{4,0},{1,5},{5,1},{2,6},{6,2},{3,7},{7,3},{8,12},{12,8},{9,1... | collective-permute-start | bytes 786440 | tf_op jit(solution)/shard_map/ppermute | solution.py:304
  54.7 1.1 %shard_map.54 = (f32[128,256]{1,0:T(8,128)S(1)}, f32[128,256]{1,0:T(8,128)S(1)}) custom-call(s32[3]{0:T(128)S(1)} %pad_add_fusion.place, f32[256,256]{1,0:T(8,128)S(1)} %get-tuple-element.93.zn.refs_4_, f32[256,256]{1,0:T(8,128)S(1)} %get-tuple-element.82.zm.refs_5_.refs_3_, f32[256,256]{1,0:T(8,128)S(1)} %get-tuple-element.83.zf.refs_4_, ...), custom_call_target="tpu_custom_call" | custom-call | flops 1000000000 | tf_op jit(solution)/shard_map/pallas_call | solution.py:279
  56.7 1.2 %shard_map.55 = (f32[128,256]{1,0:T(8,128)S(1)}, f32[128,256]{1,0:T(8,128)S(1)}) custom-call(s32[3]{0:T(128)S(1)} %pad_add_fusion.place, s32[1,6]{1,0:T(1,128)S(1)} %copy-done.3, f32[256,256]{1,0:T(8,128)S(1)} %collective-permute-done.15.refs_1_, f32[256,256]{1,0:T(8,128)S(1)} %get-tuple-element.100.refs_2_, f32[128,256]{1,0:T(8,128)S(1)} %get-tuple-element.101.refs_3_, ...), custom_call_target="tpu_custom_call" | custom-call | flops 1000000000 | tf_op jit(solution)/shard_map/pallas_call | solution.py:279
  57.9 1.9 %shard_map.56 = f32[128,768]{1,0:T(8,128)} custom-call(s32[3]{0:T(128)S(1)} %pad_add_fusion.place, s32[1,6]{1,0:T(1,128)S(1)} %copy-done.3, f32[256,256]{1,0:T(8,128)S(1)} %collective-permute-done.16.refs_0_, f32[256,256]{1,0:T(8,128)S(1)} %get-tuple-element.94.refs_1_, f32[128,256]{1,0:T(8,128)S(1)} %get-tuple-element.95.refs_2_, ...), custom_call_target="tpu_custom_call" | custom-call | flops 1000000000 | tf_op jit(solution)/shard_map/pallas_call | solution.py:279
  (43 shorter events, 13.8 us)
Async XLA Ops:
  0.0 4.4 %collective-permute-start.1 = (f32[128,768]{1,0:T(8,128)}, f32[128,768]{1,0:T(8,128)S(1)}, u32[]{:S(2)}, u32[]{:S(2)}) collective-permute-start(f32[128,768]{1,0:T(8,128)} %s_own.3), channel_id=1, source_target_pairs={{0,4},{4,0},{1,5},{5,1},{2,6},{6,2},{3,7},{7,3},{8,12},{12,8},{9,1... | collective-permute-start | bytes 1179656 | tf_op jit(solution)/shard_map/ppermute | solution.py:304
  0.7 3.7 %collective-permute-start = (s32[1,6]{1,0:T(1,128)}, s32[1,6]{1,0:T(1,128)S(1)}, u32[]{:S(2)}, u32[]{:S(2)}) collective-permute-start(s32[1,6]{1,0:T(1,128)} %pat_own.5), channel_id=1, source_target_pairs={{0,4},{4,0},{1,5},{5,1},{2,6},{6,2},{3,7},{7,3},{8,12},{12,8},{9,1... | collective-permute-start | bytes 80 | tf_op jit(solution)/shard_map/ppermute | solution.py:304
  0.7 3.7 %collective-permute-start.2 = (f32[128,384]{1,0:T(8,128)}, f32[128,384]{1,0:T(8,128)S(1)}, u32[]{:S(2)}, u32[]{:S(2)}) collective-permute-start(f32[128,384]{1,0:T(8,128)} %h_own.1), channel_id=1, source_target_pairs={{0,4},{4,0},{1,5},{5,1},{2,6},{6,2},{3,7},{7,3},{8,12},{12,8},{9,1... | collective-permute-start | bytes 589832 | tf_op jit(solution)/shard_map/ppermute | solution.py:304
  1.2 0.7 %copy-start.3 = (s32[1,6]{1,0:T(1,128)S(1)}, s32[1,6]{1,0:T(1,128)}, u32[]{:S(2)}) copy-start(s32[1,6]{1,0:T(1,128)} %pat_own.5) | copy-start | bytes 76
  1.8 1.0 %copy-start = (f32[128,768]{1,0:T(8,128)S(1)}, f32[128,768]{1,0:T(8,128)}, u32[]{:S(2)}) copy-start(f32[128,768]{1,0:T(8,128)} %s_own.3) | copy-start | bytes 1179652
  2.8 0.9 %copy-start.2 = (f32[128,384]{1,0:T(8,128)S(1)}, f32[128,384]{1,0:T(8,128)}, u32[]{:S(2)}) copy-start(f32[128,384]{1,0:T(8,128)} %h_own.1) | copy-start | bytes 589828
  4.4 7.9 %copy-start.1 = (f32[128,768]{1,0:T(8,128)S(1)}, f32[128,768]{1,0:T(8,128)}, u32[]{:S(2)}) copy-start(f32[128,768]{1,0:T(8,128)} %s_own.3) | copy-start | bytes 1179652
  5.0 4.2 %collective-permute-start.5 = (f32[128,640]{1,0:T(8,128)S(1)}, f32[128,640]{1,0:T(8,128)S(1)}, u32[]{:S(2)}, u32[]{:S(2)}) collective-permute-start(f32[128,640]{1,0:T(8,128)S(1)} %get-tuple-element.58), channel_id=1, source_target_pairs={{0,1},{1,2},{2,3},{3,7},{5,4},{6,5},{7,6},{4,0},{8,9},{9,10},{10,1... | collective-permute-start | bytes 983048 | tf_op jit(solution)/shard_map/ppermute | solution.py:307
  9.2 9.0 %collective-permute-start.6 = (f32[128,640]{1,0:T(8,128)S(1)}, f32[128,640]{1,0:T(8,128)S(1)}, u32[]{:S(2)}, u32[]{:S(2)}) collective-permute-start(f32[128,640]{1,0:T(8,128)S(1)} %collective-permute-done.5.s_got.z_got), channel_id=1, source_target_pairs={{0,4},{4,0},{1,5},{5,1},{2,6},{6,2},{3,7},{7,3},{8,12},{12,8},{9,1... | collective-permute-start | bytes 983048 | tf_op jit(solution)/shard_map/ppermute | solution.py:304
  12.1 2.1 %collective-permute-start.3 = (f32[128,256]{1,0:T(8,128)S(1)}, f32[128,256]{1,0:T(8,128)S(1)}, u32[]{:S(2)}, u32[]{:S(2)}) collective-permute-start(f32[128,256]{1,0:T(8,128)S(1)} %get-tuple-element.57), channel_id=1, source_target_pairs={{0,1},{1,2},{2,3},{3,7},{5,4},{6,5},{7,6},{4,0},{8,9},{9,10},{10,1... | collective-permute-start | bytes 393224 | tf_op jit(solution)/shard_map/ppermute | solution.py:307
  14.2 5.6 %collective-permute-start.4 = (f32[128,256]{1,0:T(8,128)S(1)}, f32[128,256]{1,0:T(8,128)S(1)}, u32[]{:S(2)}, u32[]{:S(2)}) collective-permute-start(f32[128,256]{1,0:T(8,128)S(1)} %collective-permute-done.3.z_got), channel_id=1, source_target_pairs={{0,4},{4,0},{1,5},{5,1},{2,6},{6,2},{3,7},{7,3},{8,12},{12,8},{9,1... | collective-permute-start | bytes 393224 | tf_op jit(solution)/shard_map/ppermute | solution.py:304
  19.6 2.8 %collective-permute-start.9 = (f32[128,384]{1,0:T(8,128)S(1)}, f32[128,384]{1,0:T(8,128)S(1)}, u32[]{:S(2)}, u32[]{:S(2)}) collective-permute-start(f32[128,384]{1,0:T(8,128)S(1)} %get-tuple-element.70), channel_id=1, source_target_pairs={{0,1},{1,2},{2,3},{3,7},{5,4},{6,5},{7,6},{4,0},{8,9},{9,10},{10,1... | collective-permute-start | bytes 589832 | tf_op jit(solution)/shard_map/ppermute | solution.py:307
  20.6 5.6 %collective-permute-start.7 = (f32[256,256]{1,0:T(8,128)S(1)}, f32[256,256]{1,0:T(8,128)S(1)}, u32[]{:S(2)}, u32[]{:S(2)}) collective-permute-start(f32[256,256]{1,0:T(8,128)S(1)} %shard_map.42.d_far.refs_7_), channel_id=1, source_target_pairs={{0,1},{1,2},{2,3},{3,7},{5,4},{6,5},{7,6},{4,0},{8,9},{9,10},{10,1... | collective-permute-start | bytes 786440 | tf_op jit(solution)/shard_map/ppermute | solution.py:307
  22.4 7.1 %collective-permute-start.10 = (f32[128,384]{1,0:T(8,128)S(1)}, f32[128,384]{1,0:T(8,128)S(1)}, u32[]{:S(2)}, u32[]{:S(2)}) collective-permute-start(f32[128,384]{1,0:T(8,128)S(1)} %collective-permute-done.9.d_own), channel_id=1, source_target_pairs={{0,4},{4,0},{1,5},{5,1},{2,6},{6,2},{3,7},{7,3},{8,12},{12,8},{9,1... | collective-permute-start | bytes 589832 | tf_op jit(solution)/shard_map/ppermute | solution.py:304
  26.3 5.6 %collective-permute-start.8 = (f32[256,256]{1,0:T(8,128)S(1)}, f32[256,256]{1,0:T(8,128)S(1)}, u32[]{:S(2)}, u32[]{:S(2)}) collective-permute-start(f32[256,256]{1,0:T(8,128)S(1)} %collective-permute-done.7.refs_2_), channel_id=1, source_target_pairs={{0,4},{4,0},{1,5},{5,1},{2,6},{6,2},{3,7},{7,3},{8,12},{12,8},{9,1... | collective-permute-start | bytes 786440 | tf_op jit(solution)/shard_map/ppermute | solution.py:304
  33.4 3.9 %collective-permute-start.13 = (f32[256,256]{1,0:T(8,128)S(1)}, f32[256,256]{1,0:T(8,128)S(1)}, u32[]{:S(2)}, u32[]{:S(2)}) collective-permute-start(f32[256,256]{1,0:T(8,128)S(1)} %get-tuple-element.83.zf.refs_4_), channel_id=1, source_target_pairs={{0,1},{1,2},{2,3},{3,7},{5,4},{6,5},{7,6},{4,0},{8,9},{9,10},{10,1... | collective-permute-start | bytes 786440 | tf_op jit(solution)/shard_map/ppermute | solution.py:307
  33.9 6.1 %collective-permute-start.11 = (f32[256,256]{1,0:T(8,128)S(1)}, f32[256,256]{1,0:T(8,128)S(1)}, u32[]{:S(2)}, u32[]{:S(2)}) collective-permute-start(f32[256,256]{1,0:T(8,128)S(1)} %get-tuple-element.82.zm.refs_5_.refs_3_), channel_id=1, source_target_pairs={{0,1},{1,2},{2,3},{3,7},{5,4},{6,5},{7,6},{4,0},{8,9},{9,10},{10,1... | collective-permute-start | bytes 786440 | tf_op jit(solution)/shard_map/ppermute | solution.py:307
  37.2 7.6 %collective-permute-start.14 = (f32[256,256]{1,0:T(8,128)S(1)}, f32[256,256]{1,0:T(8,128)S(1)}, u32[]{:S(2)}, u32[]{:S(2)}) collective-permute-start(f32[256,256]{1,0:T(8,128)S(1)} %collective-permute-done.13.z_got), channel_id=1, source_target_pairs={{0,4},{4,0},{1,5},{5,1},{2,6},{6,2},{3,7},{7,3},{8,12},{12,8},{9,1... | collective-permute-start | bytes 786440 | tf_op jit(solution)/shard_map/ppermute | solution.py:304
  40.0 6.7 %collective-permute-start.12 = (f32[256,256]{1,0:T(8,128)S(1)}, f32[256,256]{1,0:T(8,128)S(1)}, u32[]{:S(2)}, u32[]{:S(2)}) collective-permute-start(f32[256,256]{1,0:T(8,128)S(1)} %collective-permute-done.11.z_got), channel_id=1, source_target_pairs={{0,4},{4,0},{1,5},{5,1},{2,6},{6,2},{3,7},{7,3},{8,12},{12,8},{9,1... | collective-permute-start | bytes 786440 | tf_op jit(solution)/shard_map/ppermute | solution.py:304
  46.2 3.2 %collective-permute-start.17 = (f32[128,384]{1,0:T(8,128)S(1)}, f32[128,384]{1,0:T(8,128)S(1)}, u32[]{:S(2)}, u32[]{:S(2)}) collective-permute-start(f32[128,384]{1,0:T(8,128)S(1)} %get-tuple-element.92), channel_id=1, source_target_pairs={{0,1},{1,2},{2,3},{3,7},{5,4},{6,5},{7,6},{4,0},{8,9},{9,10},{10,1... | collective-permute-start | bytes 589832 | tf_op jit(solution)/shard_map/ppermute | solution.py:307
  47.6 5.2 %collective-permute-start.15 = (f32[256,256]{1,0:T(8,128)S(1)}, f32[256,256]{1,0:T(8,128)S(1)}, u32[]{:S(2)}, u32[]{:S(2)}) collective-permute-start(f32[256,256]{1,0:T(8,128)S(1)} %shard_map.51.d_far.refs_7_), channel_id=1, source_target_pairs={{0,1},{1,2},{2,3},{3,7},{5,4},{6,5},{7,6},{4,0},{8,9},{9,10},{10,1... | collective-permute-start | bytes 786440 | tf_op jit(solution)/shard_map/ppermute | solution.py:307
  49.4 6.5 %collective-permute-start.18 = (f32[128,384]{1,0:T(8,128)S(1)}, f32[128,384]{1,0:T(8,128)S(1)}, u32[]{:S(2)}, u32[]{:S(2)}) collective-permute-start(f32[128,384]{1,0:T(8,128)S(1)} %collective-permute-done.17.d_own), channel_id=1, source_target_pairs={{0,4},{4,0},{1,5},{5,1},{2,6},{6,2},{3,7},{7,3},{8,12},{12,8},{9,1... | collective-permute-start | bytes 589832 | tf_op jit(solution)/shard_map/ppermute | solution.py:304
  52.9 5.0 %collective-permute-start.16 = (f32[256,256]{1,0:T(8,128)S(1)}, f32[256,256]{1,0:T(8,128)S(1)}, u32[]{:S(2)}, u32[]{:S(2)}) collective-permute-start(f32[256,256]{1,0:T(8,128)S(1)} %collective-permute-done.15.refs_1_), channel_id=1, source_target_pairs={{0,4},{4,0},{1,5},{5,1},{2,6},{6,2},{3,7},{7,3},{8,12},{12,8},{9,1... | collective-permute-start | bytes 786440 | tf_op jit(solution)/shard_map/ppermute | solution.py:304

commit v4 on v3

--- a/solution.py
+++ b/solution.py
@@ -64,7 +64,7 @@
     )
 
 
-def stage_kernel(place, pat_own, s_own, h_own, s_out, h_out):
+def stage_kernel(place, s_own, h_own, s_out, h_out):
     width = s_out.shape[1]
     s_out[...] = s_own[:, width:2 * width]
     h_out[...] = h_own[...]
@@ -92,7 +92,7 @@
     outs[2][...] = tn(far, z)
 
 
-def first_local_kernel(place, s_own, s_oth, h_own, h_oth, sn, sm, sf, zn, zm, zf, tn_, tm, tf):
+def first_local_kernel(place, pat_own, s_own, s_oth, h_own, h_oth, sn, sm, sf, zn, zm, zf, tn_, tm, tf):
     side = place[0]
     rows = s_own.shape[0]
     width = 2 * rows
@@ -308,12 +308,12 @@
         return got, swap(got)
 
     s_oth, h_oth, p_oth = swap(intersect), swap(half_factors), swap(z_pattern)
-    s_mid, h_own = call(stage_kernel, [(rows, width), (rows, 3 * rows)], [place, z_pattern], [intersect, half_factors])
+    s_mid, h_own = call(stage_kernel, [(rows, width), (rows, 3 * rows)], [place], [intersect, half_factors])
     off, diag = call(start_kernel, [(rows, 5 * rows), (rows, width)], [place, p_oth], [s_mid, s_oth, h_own, h_oth])
     s_near, s_far = z_near, z_far = exchange(off)
     g_near, g_far = exchange(diag)
     sn, sm, sf, zn, zm, zf, t_near, t_mid, t_far = call(
-        first_local_kernel, [square] * 9, [place], [intersect, s_oth, h_own, h_oth])
+        first_local_kernel, [square] * 9, [place, z_pattern], [intersect, s_oth, h_own, h_oth])
     for step in range(ITERS):
         final, wide = step == ITERS - 1, step > 0
         if wide:

time: 60.7 us -> 60.2 us (level)
  no operation moved by 1% of the time
where the time goes in v4:
time: 60.2 us; the launch traced here: 59.3 us
  starting transfers between devices  23.2 us (39%)
  Pallas kernels  22.4 us (37%)
  waiting for transfers between devices  11.4 us (19%)
  local copies, waits for them, and re-layouts  1.94 us (3%)
    pallas_call x20, Pallas kernels, call(): pl.pallas_call(kernel, out_shape=shapes if many else shapes[0], in_specs=...  22.4 us
    ppermute x11, starting transfers between devices, swap(): return lax.ppermute(value, 'side', [(0, 1), (1, 0)])  21 us
    ppermute x8, waiting for transfers between devices, exchange(): got = lax.ppermute(payload, ('side', 'blk'), cycle)  11.4 us
    ppermute x8, starting transfers between devices, exchange(): got = lax.ppermute(payload, ('side', 'blk'), cycle)  2.15 us
    unnamed x8, local copies, waits for them, and re-layouts  1.94 us
  transfers between devices with their start and end apart: 19, of which 6 were waited for; matrix products, arithmetic and copies ran while one was open for 0% of the time, Pallas kernels for 31%

profile of v4, /device:TPU:29, one launch (start us, length us, event | category | flops | bytes accessed | tf_op | source)
XLA Modules:
  0.0 59.3 jit_solution(8489199507945683642)
XLA Ops:
  4.6 4.0 %collective-permute-done.5.s_got.z_got = f32[128,640]{1,0:T(8,128)S(1)} collective-permute-done((f32[128,640]{1,0:T(8,128)S(1)}, f32[128,640]{1,0:T(8,128)S(1)}, u32[]{:S(2)}, u32[]{:S(2)}) %collective-permute-start.5) | collective-permute-done | bytes 327712 | tf_op jit(solution)/shard_map/ppermute | solution.py:307
  8.6 2.9 %collective-permute-start.6 = (f32[128,640]{1,0:T(8,128)S(1)}, f32[128,640]{1,0:T(8,128)S(1)}, u32[]{:S(2)}, u32[]{:S(2)}) collective-permute-start(f32[128,640]{1,0:T(8,128)S(1)} %collective-permute-done.5.s_got.z_got), channel_id=1, source_target_pairs={{0,4},{4,0},{1,5},{5,1},{2,6},{6,2},{3,7},{7,3},{8,12},{12,8},{9,1... | collective-permute-start | bytes 983048 | tf_op jit(solution)/shard_map/ppermute | solution.py:304
  11.7 1.1 %shard_map.39 = (f32[256,256]{1,0:T(8,128)S(1)}, f32[256,256]{1,0:T(8,128)S(1)}, f32[256,256]{1,0:T(8,128)S(1)}, f32[256,256]{1,0:T(8,128)S(1)}, f32[256,256]{1,...) custom-call(s32[3]{0:T(128)S(1)} %pad_add_fusion.place, ...), custom_call_target="tpu_custom_call" | custom-call | flops 1000000000 | tf_op jit(solution)/shard_map/pallas_call | solution.py:279
  13.6 2.9 %collective-permute-start.4 = (f32[128,256]{1,0:T(8,128)S(1)}, f32[128,256]{1,0:T(8,128)S(1)}, u32[]{:S(2)}, u32[]{:S(2)}) collective-permute-start(f32[128,256]{1,0:T(8,128)S(1)} %collective-permute-done.3.z_got), channel_id=1, source_target_pairs={{0,4},{4,0},{1,5},{5,1},{2,6},{6,2},{3,7},{7,3},{8,12},{12,8},{9,1... | collective-permute-start | bytes 393224 | tf_op jit(solution)/shard_map/ppermute | solution.py:304
  16.5 1.1 %shard_map.40 = (f32[256,256]{1,0:T(8,128)S(1)}, f32[256,256]{1,0:T(8,128)S(1)}, f32[256,256]{1,0:T(8,128)S(1)}) custom-call(s32[3]{0:T(128)S(1)} %pad_add_fusion.place, f32[128,640]{1,0:T(8,128)S(1)} %collective-permute-done.5.s_got.z_got, f32[128,640]{1,0:T(8,128)S(1)} %collective-permute-done.5.s_got.z_got, f32[256,256]{1,0:T(8,128)S(1)} %get-tuple-element.63.sn, ...), custom_call_target="tpu_custom_call" | custom-call | flops 1000000000 | tf_op jit(solution)/shard_map/pallas_call | solution.py:279
  17.7 1.4 %shard_map.41 = (f32[256,256]{1,0:T(8,128)S(1)}, f32[256,256]{1,0:T(8,128)S(1)}, f32[256,256]{1,0:T(8,128)S(1)}, f32[256,256]{1,0:T(8,128)S(1)}, f32[128,384]{1,0:T(8,128)S(1)}) custom-call(s32[3]{0:T(128)S(1)} %pad_add_fusion.place, f32[128,640]{1,0:T(8,128)S(1)} %collective-permute-done.6.s_got.z_got, f32[128,640]{1,0:T(8,128)S(1)} %collective-permute-done.6.s_got.z_got, ...), custom_call_target="tpu_custom_call" | custom-call | flops 1000000000 | tf_op jit(solution)/shard_map/pallas_call | solution.py:279
  20.3 1.6 %collective-permute-done.9.d_own = f32[128,384]{1,0:T(8,128)S(1)} collective-permute-done((f32[128,384]{1,0:T(8,128)S(1)}, f32[128,384]{1,0:T(8,128)S(1)}, u32[]{:S(2)}, u32[]{:S(2)}) %collective-permute-start.9) | collective-permute-done | bytes 196640 | tf_op jit(solution)/shard_map/ppermute | solution.py:307
  21.8 2.9 %collective-permute-start.10 = (f32[128,384]{1,0:T(8,128)S(1)}, f32[128,384]{1,0:T(8,128)S(1)}, u32[]{:S(2)}, u32[]{:S(2)}) collective-permute-start(f32[128,384]{1,0:T(8,128)S(1)} %collective-permute-done.9.d_own), channel_id=1, source_target_pairs={{0,4},{4,0},{1,5},{5,1},{2,6},{6,2},{3,7},{7,3},{8,12},{12,8},{9,1... | collective-permute-start | bytes 589832 | tf_op jit(solution)/shard_map/ppermute | solution.py:304
  25.7 1.8 %collective-permute-start.8 = (f32[256,256]{1,0:T(8,128)S(1)}, f32[256,256]{1,0:T(8,128)S(1)}, u32[]{:S(2)}, u32[]{:S(2)}) collective-permute-start(f32[256,256]{1,0:T(8,128)S(1)} %collective-permute-done.7.refs_2_), channel_id=1, source_target_pairs={{0,4},{4,0},{1,5},{5,1},{2,6},{6,2},{3,7},{7,3},{8,12},{12,8},{9,1... | collective-permute-start | bytes 786440 | tf_op jit(solution)/shard_map/ppermute | solution.py:304
  27.5 1.4 %shard_map.45 = (f32[256,256]{1,0:T(8,128)S(1)}, f32[256,256]{1,0:T(8,128)S(1)}) custom-call(s32[3]{0:T(128)S(1)} %pad_add_fusion.place, f32[256,256]{1,0:T(8,128)S(1)} %get-tuple-element.71.zn.refs_5_, f32[256,256]{1,0:T(8,128)S(1)} %get-tuple-element.60.zm.refs_6_.refs_3_, f32[256,256]{1,0:T(8,128)S(1)} %get-tuple-element.61.zf.refs_4_, ...), custom_call_target="tpu_custom_call" | custom-call | flops 1000000000 | tf_op jit(solution)/shard_map/pallas_call | solution.py:279
  29.9 1.4 %shard_map.46 = (f32[256,256]{1,0:T(8,128)S(1)}, f32[256,256]{1,0:T(8,128)S(1)}) custom-call(s32[3]{0:T(128)S(1)} %pad_add_fusion.place, s32[1,6]{1,0:T(1,128)S(1)} %copy-done.3, s32[1,6]{1,0:T(1,128)S(1)} %collective-permute-done.pattern.refs_1_.pat_oth, f32[256,256]{1,0:T(8,128)S(1)} %collective-permute-done.7.refs_2_, ...), custom_call_target="tpu_custom_call" | custom-call | flops 1000000000 | tf_op jit(solution)/shard_map/pallas_call | solution.py:279
  31.4 1.4 %shard_map.47 = (f32[256,256]{1,0:T(8,128)S(1)}, f32[256,256]{1,0:T(8,128)S(1)}) custom-call(s32[3]{0:T(128)S(1)} %pad_add_fusion.place, s32[1,6]{1,0:T(1,128)S(1)} %copy-done.3, s32[1,6]{1,0:T(1,128)S(1)} %collective-permute-done.pattern.refs_1_.pat_oth, f32[256,256]{1,0:T(8,128)S(1)} %collective-permute-done.8.refs_0_, ...), custom_call_target="tpu_custom_call" | custom-call | flops 1000000000 | tf_op jit(solution)/shard_map/pallas_call | solution.py:279
  33.5 3.1 %collective-permute-done.13.z_got = f32[256,256]{1,0:T(8,128)S(1)} collective-permute-done((f32[256,256]{1,0:T(8,128)S(1)}, f32[256,256]{1,0:T(8,128)S(1)}, u32[]{:S(2)}, u32[]{:S(2)}) %collective-permute-start.13) | collective-permute-done | bytes 262176 | tf_op jit(solution)/shard_map/ppermute | solution.py:307
  36.7 2.5 %collective-permute-start.14 = (f32[256,256]{1,0:T(8,128)S(1)}, f32[256,256]{1,0:T(8,128)S(1)}, u32[]{:S(2)}, u32[]{:S(2)}) collective-permute-start(f32[256,256]{1,0:T(8,128)S(1)} %collective-permute-done.13.z_got), channel_id=1, source_target_pairs={{0,4},{4,0},{1,5},{5,1},{2,6},{6,2},{3,7},{7,3},{8,12},{12,8},{9,1... | collective-permute-start | bytes 786440 | tf_op jit(solution)/shard_map/ppermute | solution.py:304
  39.5 2.5 %collective-permute-start.12 = (f32[256,256]{1,0:T(8,128)S(1)}, f32[256,256]{1,0:T(8,128)S(1)}, u32[]{:S(2)}, u32[]{:S(2)}) collective-permute-start(f32[256,256]{1,0:T(8,128)S(1)} %collective-permute-done.11.z_got), channel_id=1, source_target_pairs={{0,4},{4,0},{1,5},{5,1},{2,6},{6,2},{3,7},{7,3},{8,12},{12,8},{9,1... | collective-permute-start | bytes 786440 | tf_op jit(solution)/shard_map/ppermute | solution.py:304
  42.0 1.1 %shard_map.48 = (f32[256,256]{1,0:T(8,128)S(1)}, f32[256,256]{1,0:T(8,128)S(1)}, f32[256,256]{1,0:T(8,128)S(1)}) custom-call(s32[3]{0:T(128)S(1)} %pad_add_fusion.place, f32[256,256]{1,0:T(8,128)S(1)} %get-tuple-element.63.sn, f32[256,256]{1,0:T(8,128)S(1)} %get-tuple-element.84.sm, f32[256,256]{1,0:T(8,128)S(1)} %get-tuple-element.59.sf, ...), custom_call_target="tpu_custom_call" | custom-call | flops 1000000000 | tf_op jit(solution)/shard_map/pallas_call | solution.py:279
  43.1 1.2 %shard_map.49 = (f32[256,256]{1,0:T(8,128)S(1)}, f32[256,256]{1,0:T(8,128)S(1)}, f32[256,256]{1,0:T(8,128)S(1)}) custom-call(s32[3]{0:T(128)S(1)} %pad_add_fusion.place, f32[128,640]{1,0:T(8,128)S(1)} %collective-permute-done.5.s_got.z_got, f32[256,256]{1,0:T(8,128)S(1)} %collective-permute-done.13.z_got, f32[256,256]{1,0:T(8,128)S(1)} %get-tuple-element.63.sn, ...), custom_call_target="tpu_custom_call" | custom-call | flops 1000000000 | tf_op jit(solution)/shard_map/pallas_call | solution.py:279
  44.3 1.4 %shard_map.50 = (f32[256,256]{1,0:T(8,128)S(1)}, f32[256,256]{1,0:T(8,128)S(1)}, f32[256,256]{1,0:T(8,128)S(1)}, f32[256,256]{1,0:T(8,128)S(1)}, f32[128,384]{1,0:T(8,128)S(1)}) custom-call(s32[3]{0:T(128)S(1)} %pad_add_fusion.place, f32[128,640]{1,0:T(8,128)S(1)} %collective-permute-done.6.s_got.z_got, f32[256,256]{1,0:T(8,128)S(1)} %collective-permute-done.14.z_got, ...), custom_call_target="tpu_custom_call" | custom-call | flops 1000000000 | tf_op jit(solution)/shard_map/pallas_call | solution.py:279
  47.2 1.6 %collective-permute-done.17.d_own = f32[128,384]{1,0:T(8,128)S(1)} collective-permute-done((f32[128,384]{1,0:T(8,128)S(1)}, f32[128,384]{1,0:T(8,128)S(1)}, u32[]{:S(2)}, u32[]{:S(2)}) %collective-permute-start.17) | collective-permute-done | bytes 196640 | tf_op jit(solution)/shard_map/ppermute | solution.py:307
  48.8 2.5 %collective-permute-start.18 = (f32[128,384]{1,0:T(8,128)S(1)}, f32[128,384]{1,0:T(8,128)S(1)}, u32[]{:S(2)}, u32[]{:S(2)}) collective-permute-start(f32[128,384]{1,0:T(8,128)S(1)} %collective-permute-done.17.d_own), channel_id=1, source_target_pairs={{0,4},{4,0},{1,5},{5,1},{2,6},{6,2},{3,7},{7,3},{8,12},{12,8},{9,1... | collective-permute-start | bytes 589832 | tf_op jit(solution)/shard_map/ppermute | solution.py:304
  52.3 1.8 %collective-permute-start.16 = (f32[256,256]{1,0:T(8,128)S(1)}, f32[256,256]{1,0:T(8,128)S(1)}, u32[]{:S(2)}, u32[]{:S(2)}) collective-permute-start(f32[256,256]{1,0:T(8,128)S(1)} %collective-permute-done.15.refs_1_), channel_id=1, source_target_pairs={{0,4},{4,0},{1,5},{5,1},{2,6},{6,2},{3,7},{7,3},{8,12},{12,8},{9,1... | collective-permute-start | bytes 786440 | tf_op jit(solution)/shard_map/ppermute | solution.py:304
  54.2 1.1 %shard_map.54 = (f32[128,256]{1,0:T(8,128)S(1)}, f32[128,256]{1,0:T(8,128)S(1)}) custom-call(s32[3]{0:T(128)S(1)} %pad_add_fusion.place, f32[256,256]{1,0:T(8,128)S(1)} %get-tuple-element.93.zn.refs_4_, f32[256,256]{1,0:T(8,128)S(1)} %get-tuple-element.82.zm.refs_5_.refs_3_, f32[256,256]{1,0:T(8,128)S(1)} %get-tuple-element.83.zf.refs_4_, ...), custom_call_target="tpu_custom_call" | custom-call | flops 1000000000 | tf_op jit(solution)/shard_map/pallas_call | solution.py:279
  56.2 1.2 %shard_map.55 = (f32[128,256]{1,0:T(8,128)S(1)}, f32[128,256]{1,0:T(8,128)S(1)}) custom-call(s32[3]{0:T(128)S(1)} %pad_add_fusion.place, s32[1,6]{1,0:T(1,128)S(1)} %copy-done.3, f32[256,256]{1,0:T(8,128)S(1)} %collective-permute-done.15.refs_1_, f32[256,256]{1,0:T(8,128)S(1)} %get-tuple-element.100.refs_2_, f32[128,256]{1,0:T(8,128)S(1)} %get-tuple-element.101.refs_3_, ...), custom_call_target="tpu_custom_call" | custom-call | flops 1000000000 | tf_op jit(solution)/shard_map/pallas_call | solution.py:279
  57.4 1.9 %shard_map.56 = f32[128,768]{1,0:T(8,128)} custom-call(s32[3]{0:T(128)S(1)} %pad_add_fusion.place, s32[1,6]{1,0:T(1,128)S(1)} %copy-done.3, f32[256,256]{1,0:T(8,128)S(1)} %collective-permute-done.16.refs_0_, f32[256,256]{1,0:T(8,128)S(1)} %get-tuple-element.94.refs_1_, f32[128,256]{1,0:T(8,128)S(1)} %get-tuple-element.95.refs_2_, ...), custom_call_target="tpu_custom_call" | custom-call | flops 1000000000 | tf_op jit(solution)/shard_map/pallas_call | solution.py:279
  (43 shorter events, 13.2 us)
Async XLA Ops:
  0.0 3.8 %collective-permute-start.1 = (f32[128,768]{1,0:T(8,128)}, f32[128,768]{1,0:T(8,128)S(1)}, u32[]{:S(2)}, u32[]{:S(2)}) collective-permute-start(f32[128,768]{1,0:T(8,128)} %s_own.3), channel_id=1, source_target_pairs={{0,4},{4,0},{1,5},{5,1},{2,6},{6,2},{3,7},{7,3},{8,12},{12,8},{9,1... | collective-permute-start | bytes 1179656 | tf_op jit(solution)/shard_map/ppermute | solution.py:304
  0.7 3.1 %collective-permute-start = (s32[1,6]{1,0:T(1,128)}, s32[1,6]{1,0:T(1,128)S(1)}, u32[]{:S(2)}, u32[]{:S(2)}) collective-permute-start(s32[1,6]{1,0:T(1,128)} %pat_own.5), channel_id=1, source_target_pairs={{0,4},{4,0},{1,5},{5,1},{2,6},{6,2},{3,7},{7,3},{8,12},{12,8},{9,1... | collective-permute-start | bytes 80 | tf_op jit(solution)/shard_map/ppermute | solution.py:304
  0.7 3.1 %collective-permute-start.2 = (f32[128,384]{1,0:T(8,128)}, f32[128,384]{1,0:T(8,128)S(1)}, u32[]{:S(2)}, u32[]{:S(2)}) collective-permute-start(f32[128,384]{1,0:T(8,128)} %h_own.1), channel_id=1, source_target_pairs={{0,4},{4,0},{1,5},{5,1},{2,6},{6,2},{3,7},{7,3},{8,12},{12,8},{9,1... | collective-permute-start | bytes 589832 | tf_op jit(solution)/shard_map/ppermute | solution.py:304
  1.3 1.0 %copy-start = (f32[128,768]{1,0:T(8,128)S(1)}, f32[128,768]{1,0:T(8,128)}, u32[]{:S(2)}) copy-start(f32[128,768]{1,0:T(8,128)} %s_own.3) | copy-start | bytes 1179652
  2.3 0.9 %copy-start.2 = (f32[128,384]{1,0:T(8,128)S(1)}, f32[128,384]{1,0:T(8,128)}, u32[]{:S(2)}) copy-start(f32[128,384]{1,0:T(8,128)} %h_own.1) | copy-start | bytes 589828
  3.8 7.9 %copy-start.1 = (f32[128,768]{1,0:T(8,128)S(1)}, f32[128,768]{1,0:T(8,128)}, u32[]{:S(2)}) copy-start(f32[128,768]{1,0:T(8,128)} %s_own.3) | copy-start | bytes 1179652
  4.4 7.3 %copy-start.3 = (s32[1,6]{1,0:T(1,128)S(1)}, s32[1,6]{1,0:T(1,128)}, u32[]{:S(2)}) copy-start(s32[1,6]{1,0:T(1,128)} %pat_own.5) | copy-start | bytes 76
  4.4 4.2 %collective-permute-start.5 = (f32[128,640]{1,0:T(8,128)S(1)}, f32[128,640]{1,0:T(8,128)S(1)}, u32[]{:S(2)}, u32[]{:S(2)}) collective-permute-start(f32[128,640]{1,0:T(8,128)S(1)} %get-tuple-element.58), channel_id=1, source_target_pairs={{0,1},{1,2},{2,3},{3,7},{5,4},{6,5},{7,6},{4,0},{8,9},{9,10},{10,1... | collective-permute-start | bytes 983048 | tf_op jit(solution)/shard_map/ppermute | solution.py:307
  8.6 9.0 %collective-permute-start.6 = (f32[128,640]{1,0:T(8,128)S(1)}, f32[128,640]{1,0:T(8,128)S(1)}, u32[]{:S(2)}, u32[]{:S(2)}) collective-permute-start(f32[128,640]{1,0:T(8,128)S(1)} %collective-permute-done.5.s_got.z_got), channel_id=1, source_target_pairs={{0,4},{4,0},{1,5},{5,1},{2,6},{6,2},{3,7},{7,3},{8,12},{12,8},{9,1... | collective-permute-start | bytes 983048 | tf_op jit(solution)/shard_map/ppermute | solution.py:304
  11.5 2.1 %collective-permute-start.3 = (f32[128,256]{1,0:T(8,128)S(1)}, f32[128,256]{1,0:T(8,128)S(1)}, u32[]{:S(2)}, u32[]{:S(2)}) collective-permute-start(f32[128,256]{1,0:T(8,128)S(1)} %get-tuple-element.57), channel_id=1, source_target_pairs={{0,1},{1,2},{2,3},{3,7},{5,4},{6,5},{7,6},{4,0},{8,9},{9,10},{10,1... | collective-permute-start | bytes 393224 | tf_op jit(solution)/shard_map/ppermute | solution.py:307
  13.6 5.6 %collective-permute-start.4 = (f32[128,256]{1,0:T(8,128)S(1)}, f32[128,256]{1,0:T(8,128)S(1)}, u32[]{:S(2)}, u32[]{:S(2)}) collective-permute-start(f32[128,256]{1,0:T(8,128)S(1)} %collective-permute-done.3.z_got), channel_id=1, source_target_pairs={{0,4},{4,0},{1,5},{5,1},{2,6},{6,2},{3,7},{7,3},{8,12},{12,8},{9,1... | collective-permute-start | bytes 393224 | tf_op jit(solution)/shard_map/ppermute | solution.py:304
  19.0 2.8 %collective-permute-start.9 = (f32[128,384]{1,0:T(8,128)S(1)}, f32[128,384]{1,0:T(8,128)S(1)}, u32[]{:S(2)}, u32[]{:S(2)}) collective-permute-start(f32[128,384]{1,0:T(8,128)S(1)} %get-tuple-element.70), channel_id=1, source_target_pairs={{0,1},{1,2},{2,3},{3,7},{5,4},{6,5},{7,6},{4,0},{8,9},{9,10},{10,1... | collective-permute-start | bytes 589832 | tf_op jit(solution)/shard_map/ppermute | solution.py:307
  20.1 5.7 %collective-permute-start.7 = (f32[256,256]{1,0:T(8,128)S(1)}, f32[256,256]{1,0:T(8,128)S(1)}, u32[]{:S(2)}, u32[]{:S(2)}) collective-permute-start(f32[256,256]{1,0:T(8,128)S(1)} %shard_map.42.d_far.refs_7_), channel_id=1, source_target_pairs={{0,1},{1,2},{2,3},{3,7},{5,4},{6,5},{7,6},{4,0},{8,9},{9,10},{10,1... | collective-permute-start | bytes 786440 | tf_op jit(solution)/shard_map/ppermute | solution.py:307
  21.8 7.1 %collective-permute-start.10 = (f32[128,384]{1,0:T(8,128)S(1)}, f32[128,384]{1,0:T(8,128)S(1)}, u32[]{:S(2)}, u32[]{:S(2)}) collective-permute-start(f32[128,384]{1,0:T(8,128)S(1)} %collective-permute-done.9.d_own), channel_id=1, source_target_pairs={{0,4},{4,0},{1,5},{5,1},{2,6},{6,2},{3,7},{7,3},{8,12},{12,8},{9,1... | collective-permute-start | bytes 589832 | tf_op jit(solution)/shard_map/ppermute | solution.py:304
  25.7 5.6 %collective-permute-start.8 = (f32[256,256]{1,0:T(8,128)S(1)}, f32[256,256]{1,0:T(8,128)S(1)}, u32[]{:S(2)}, u32[]{:S(2)}) collective-permute-start(f32[256,256]{1,0:T(8,128)S(1)} %collective-permute-done.7.refs_2_), channel_id=1, source_target_pairs={{0,4},{4,0},{1,5},{5,1},{2,6},{6,2},{3,7},{7,3},{8,12},{12,8},{9,1... | collective-permute-start | bytes 786440 | tf_op jit(solution)/shard_map/ppermute | solution.py:304
  32.8 3.8 %collective-permute-start.13 = (f32[256,256]{1,0:T(8,128)S(1)}, f32[256,256]{1,0:T(8,128)S(1)}, u32[]{:S(2)}, u32[]{:S(2)}) collective-permute-start(f32[256,256]{1,0:T(8,128)S(1)} %get-tuple-element.83.zf.refs_4_), channel_id=1, source_target_pairs={{0,1},{1,2},{2,3},{3,7},{5,4},{6,5},{7,6},{4,0},{8,9},{9,10},{10,1... | collective-permute-start | bytes 786440 | tf_op jit(solution)/shard_map/ppermute | solution.py:307
  33.3 6.1 %collective-permute-start.11 = (f32[256,256]{1,0:T(8,128)S(1)}, f32[256,256]{1,0:T(8,128)S(1)}, u32[]{:S(2)}, u32[]{:S(2)}) collective-permute-start(f32[256,256]{1,0:T(8,128)S(1)} %get-tuple-element.82.zm.refs_5_.refs_3_), channel_id=1, source_target_pairs={{0,1},{1,2},{2,3},{3,7},{5,4},{6,5},{7,6},{4,0},{8,9},{9,10},{10,1... | collective-permute-start | bytes 786440 | tf_op jit(solution)/shard_map/ppermute | solution.py:307
  36.7 7.6 %collective-permute-start.14 = (f32[256,256]{1,0:T(8,128)S(1)}, f32[256,256]{1,0:T(8,128)S(1)}, u32[]{:S(2)}, u32[]{:S(2)}) collective-permute-start(f32[256,256]{1,0:T(8,128)S(1)} %collective-permute-done.13.z_got), channel_id=1, source_target_pairs={{0,4},{4,0},{1,5},{5,1},{2,6},{6,2},{3,7},{7,3},{8,12},{12,8},{9,1... | collective-permute-start | bytes 786440 | tf_op jit(solution)/shard_map/ppermute | solution.py:304
  39.5 6.7 %collective-permute-start.12 = (f32[256,256]{1,0:T(8,128)S(1)}, f32[256,256]{1,0:T(8,128)S(1)}, u32[]{:S(2)}, u32[]{:S(2)}) collective-permute-start(f32[256,256]{1,0:T(8,128)S(1)} %collective-permute-done.11.z_got), channel_id=1, source_target_pairs={{0,4},{4,0},{1,5},{5,1},{2,6},{6,2},{3,7},{7,3},{8,12},{12,8},{9,1... | collective-permute-start | bytes 786440 | tf_op jit(solution)/shard_map/ppermute | solution.py:304
  45.7 3.2 %collective-permute-start.17 = (f32[128,384]{1,0:T(8,128)S(1)}, f32[128,384]{1,0:T(8,128)S(1)}, u32[]{:S(2)}, u32[]{:S(2)}) collective-permute-start(f32[128,384]{1,0:T(8,128)S(1)} %get-tuple-element.92), channel_id=1, source_target_pairs={{0,1},{1,2},{2,3},{3,7},{5,4},{6,5},{7,6},{4,0},{8,9},{9,10},{10,1... | collective-permute-start | bytes 589832 | tf_op jit(solution)/shard_map/ppermute | solution.py:307
  47.1 5.2 %collective-permute-start.15 = (f32[256,256]{1,0:T(8,128)S(1)}, f32[256,256]{1,0:T(8,128)S(1)}, u32[]{:S(2)}, u32[]{:S(2)}) collective-permute-start(f32[256,256]{1,0:T(8,128)S(1)} %shard_map.51.d_far.refs_7_), channel_id=1, source_target_pairs={{0,1},{1,2},{2,3},{3,7},{5,4},{6,5},{7,6},{4,0},{8,9},{9,10},{10,1... | collective-permute-start | bytes 786440 | tf_op jit(solution)/shard_map/ppermute | solution.py:307
  48.8 6.5 %collective-permute-start.18 = (f32[128,384]{1,0:T(8,128)S(1)}, f32[128,384]{1,0:T(8,128)S(1)}, u32[]{:S(2)}, u32[]{:S(2)}) collective-permute-start(f32[128,384]{1,0:T(8,128)S(1)} %collective-permute-done.17.d_own), channel_id=1, source_target_pairs={{0,4},{4,0},{1,5},{5,1},{2,6},{6,2},{3,7},{7,3},{8,12},{12,8},{9,1... | collective-permute-start | bytes 589832 | tf_op jit(solution)/shard_map/ppermute | solution.py:304
  52.3 5.0 %collective-permute-start.16 = (f32[256,256]{1,0:T(8,128)S(1)}, f32[256,256]{1,0:T(8,128)S(1)}, u32[]{:S(2)}, u32[]{:S(2)}) collective-permute-start(f32[256,256]{1,0:T(8,128)S(1)} %collective-permute-done.15.refs_1_), channel_id=1, source_target_pairs={{0,4},{4,0},{1,5},{5,1},{2,6},{6,2},{3,7},{7,3},{8,12},{12,8},{9,1... | collective-permute-start | bytes 786440 | tf_op jit(solution)/shard_map/ppermute | solution.py:304
